TPU v7x, 32 devices: a whole 2x2x4 slice. The times are simulated.
32 devices in a mesh: rows: 8 (over z, x), feat: 4 (over y, core).
Axes of the slice: x: 2, y: 2, z: 4, core: 2. Of those that a mesh axis runs over, the one named last changes fastest.
Arguments:
- tile_values: bfloat16 [2048, 256, 128], P('rows', 'feat'), may hold values from -6 to 6
- tile_blocks: int32 [2048, 256], P('rows', 'feat'), may hold values from 0 to 2047
- tile_counts: int32 [2048, 4], P('rows', 'feat'), may hold values from 1 to 64, as said below
- labels: int32 [2048], P('rows'), may hold values 0 or 1
- owner_rank: int32 [2048], P('rows'), may hold values from 0 to 7, as said below
- weights: float32 [8192, 128], P(('feat', 'rows')), may hold values from -0.09375 to 0.09375
Outputs:
- owned_margins: float32 [2048], P('rows')
- gradient: float32 [8192, 128], P(('feat', 'rows'))
- loss: float32 [], replicated
Inputs may be any that keep to these rules, and one draw needn't show every extreme that they name: `owner_rank`: within each aligned block of 256 examples, every owner is named by exactly 32 examples. `tile_counts`: in every aligned block of 256 examples, each shard's column holds at least one example with exactly 64 used slots.
All inputs are finite; a program needn't handle non-finite values. No bound on the sum of `labels` on one device may be relied on, other than what follows from the above.
Results may differ from a plain program's by a relative error of at most 0.003.
Values may be sent and summed in bfloat16 or wider, within the bound.
A program may use at most 64 MiB of HBM per device.

v0:
```python
import functools

import jax
import jax.numpy as jnp
from jax import lax
from jax.experimental import pallas as pl
from jax.experimental.pallas import tpu as pltpu
from jax.sharding import PartitionSpec as P

MESH = pl.DeviceIdType.MESH
LANES = 128
GRAIN = 16
GROUP = 32
GRANT = 24 * 1024 * 1024
COST = pl.CostEstimate(flops=0, bytes_accessed=24 * 1024 * 1024, transcendentals=0)
CHUNK = 256
NT = (((1,), (1,)), ((), ()))
NN = (((1,), (0,)), ((), ()))
VM = pl.BlockSpec(memory_space=pltpu.VMEM)
SM = pl.BlockSpec(memory_space=pltpu.SMEM)


def seat(n):
    me = lax.axis_index("rows")
    side = lax.rem(me, 2)
    partner = me + 1 - 2 * side
    column = [lax.rem(me + 2 * k, n) for k in range(n // 2)]
    source = [lax.rem(me + n - 2 * k, n) for k in range(n // 2)]
    return me, partner, column, source


def greet(axis, peers):
    barrier = pltpu.get_barrier_semaphore()
    for peer in peers:
        pl.semaphore_signal(barrier, inc=1, device_id={axis: peer}, device_id_type=MESH)
    pl.semaphore_wait(barrier, len(peers))


def send_to(axis, peer, source, target, send, recv):
    copy = pltpu.make_async_remote_copy(
        src_ref=source,
        dst_ref=target,
        send_sem=send,
        recv_sem=recv,
        device_id={axis: peer},
        device_id_type=MESH,
    )
    copy.start()
    return copy


def gather_kernel(n, w_ref, table_ref, half, send, recv, xsend, xrecv):
    half[...] = w_ref[...].astype(jnp.bfloat16)
    me, partner, column, source = seat(n)
    deep = n // 2
    greet("rows", [partner] + column[1:])
    across = [send_to("rows", partner, half, table_ref.at[me], xsend.at[0], xrecv.at[0])]
    along = [
        send_to("rows", column[k], half, table_ref.at[me], send.at[k - 1], recv.at[k - 1])
        for k in range(1, deep)
    ]
    table_ref[me] = w_ref[...].astype(jnp.bfloat16)
    for k in range(1, deep):
        along[k - 1].wait_recv()
        block = table_ref.at[source[k]]
        across.append(send_to("rows", partner, block, block, xsend.at[k], xrecv.at[k]))
    for copy in along:
        copy.wait_send()
    for copy in across:
        copy.wait()


def lane_group():
    return lax.broadcasted_iota(jnp.int32, (1, LANES), 1) // GRAIN


def group_values(vals_ref, glist, base):
    return jnp.concatenate([vals_ref[glist[base + i]] for i in range(GROUP)], axis=0)


def group_offsets(idt, rlist, base):
    group = lane_group()
    per = LANES // GRAIN
    parts = []
    for h in range(GROUP // per):
        row = idt[pl.ds(rlist[base + h * per], 1), :]
        for i in range(1, per):
            row = jnp.where(group == i, idt[pl.ds(rlist[base + h * per + i], 1), :], row)
        parts.append(row)
    ids = jnp.concatenate(parts, axis=1)
    width = GROUP * GRAIN
    return jnp.broadcast_to(ids, (8, width)) - lax.broadcasted_iota(jnp.int32, (8, width), 0)


def margin_kernel(counts, used_ref, ids_ref, table_ref, vals_ref, glist, rlist, nb, idt, partial_ref, terms):
    slots, ex = ids_ref.shape
    grains = slots // GRAIN
    live = lax.broadcasted_iota(jnp.int32, (slots, ex), 0) < used_ref[...]
    shifted = jnp.where(live, ids_ref[...] + 1, 0)
    if slots < LANES:
        shifted = jnp.concatenate([shifted, jnp.zeros((LANES - slots, ex), jnp.int32)], axis=0)
    shifted = shifted.T
    lane = lax.broadcasted_iota(jnp.int32, (ex, LANES), 1) // GRAIN
    for q in range(grains):
        piece = jnp.where(lane == q, shifted, 0)
        step = GRAIN
        while step < LANES:
            piece = piece + pltpu.roll(piece, step, 1)
            step *= 2
        idt[q * ex : (q + 1) * ex, :] = piece - 1
    idt[grains * ex :, :] = jnp.full((8, LANES), -1, jnp.int32)

    def fill(e, off):
        for q in range(grains):
            glist[off + q] = e * grains + q
            rlist[off + q] = e + q * ex
        return off + (counts[e] + (GRAIN - 1)) // GRAIN

    total = lax.fori_loop(0, ex, fill, jnp.int32(0), unroll=8)
    for i in range(GROUP):
        glist[total + i] = 0
        rlist[total + i] = grains * ex
    turns = (total + (GROUP - 1)) // GROUP
    nb[0] = turns
    terms[...] = jnp.zeros_like(terms)
    group = lane_group()
    width = GROUP * GRAIN
    per = LANES // GRAIN

    def turn(t, carry):
        base = t * GROUP
        values = group_values(vals_ref, glist, base)
        offset = group_offsets(idt, rlist, base)
        found = jnp.zeros((8, width), jnp.float32)
        for c in range(table_ref.shape[0] // CHUNK):
            scores = lax.dot_general(
                table_ref[c * CHUNK : (c + 1) * CHUNK, :], values, NT, preferred_element_type=jnp.float32
            )
            for i in range(CHUNK // 8):
                found = jnp.where(offset == c * CHUNK + i * 8, scores[i * 8 : i * 8 + 8, :], found)
        term = jnp.sum(found, axis=0, keepdims=True)
        for i in range(GROUP):
            h = i // per
            mine = jnp.where(group == i % per, term[:, h * LANES : (h + 1) * LANES], 0.0)
            terms[pl.ds(rlist[base + i], 1), :] = mine
        return carry

    lax.fori_loop(0, turns, turn, jnp.int32(0))
    spread = terms[0:ex, :]
    for q in range(1, grains):
        spread = spread + terms[q * ex : (q + 1) * ex, :]
    partial_ref[...] = jnp.broadcast_to(jnp.sum(spread.T, axis=0, keepdims=True), partial_ref.shape)


def residual_kernel(n, partial_ref, labels_ref, margin_ref, resid_ref, loss_ref, held, send, recv):
    me = lax.axis_index("feat")
    peers = [lax.rem(me + k, n) for k in range(1, n)]
    greet("feat", peers)
    copies = [
        send_to("feat", peer, partial_ref, held.at[me], send.at[k], recv.at[k])
        for k, peer in enumerate(peers)
    ]
    held[me] = partial_ref[...]
    for copy in copies:
        copy.wait()
    margin = held[0]
    for k in range(1, n):
        margin = margin + held[k]
    label = labels_ref[...].astype(jnp.float32)
    residual = 1.0 / (1.0 + jnp.exp(-margin)) - label
    margin_ref[...] = margin
    resid_ref[...] = residual.astype(jnp.bfloat16).astype(jnp.float32)[0:1, :]
    term = jnp.maximum(margin, 0.0) + jnp.log1p(jnp.exp(-jnp.abs(margin))) - label * margin
    total = term[:, 0:LANES]
    for h in range(1, term.shape[1] // LANES):
        total = total + term[:, h * LANES : (h + 1) * LANES]
    loss_ref[...] = total


def gradient_kernel(grains, glist, rlist, nb, resid, idt, vals_ref, out_ref, total):
    total[...] = jnp.zeros_like(total)
    group = lane_group()
    width = GROUP * GRAIN
    per = LANES // GRAIN

    def turn(t, carry):
        base = t * GROUP
        values = group_values(vals_ref, glist, base)
        offset = group_offsets(idt, rlist, base)
        parts = []
        for h in range(GROUP // per):
            row = jnp.zeros((1, LANES), jnp.float32)
            for i in range(per):
                row = jnp.where(group == i, resid[0, glist[base + h * per + i] // grains], row)
            parts.append(row)
        factor = jnp.broadcast_to(jnp.concatenate(parts, axis=1), (8, width))
        for c in range(total.shape[0] // CHUNK):
            spread = jnp.concatenate(
                [jnp.where(offset == c * CHUNK + i * 8, factor, 0.0) for i in range(CHUNK // 8)], axis=0
            ).astype(jnp.bfloat16)
            total[c * CHUNK : (c + 1) * CHUNK, :] += lax.dot_general(
                spread, values, NN, preferred_element_type=jnp.float32
            )
        return carry

    lax.fori_loop(0, nb[0], turn, jnp.int32(0))
    out_ref[...] = total[...].astype(jnp.bfloat16)


def scatter_kernel(n, grad_ref, margin_ref, owner_ref, loss_ref, sum_ref, notes_ref, notes, crossed, paired, held, send, recv, xsend, xrecv, nsend, nrecv):
    ex = margin_ref.shape[1]
    owner = owner_ref[...].astype(jnp.float32)
    square = jnp.broadcast_to(owner, (ex, ex))
    earlier = lax.broadcasted_iota(jnp.int32, (ex, ex), 0) < lax.broadcasted_iota(jnp.int32, (ex, ex), 1)
    same = jnp.where(jnp.logical_and(square.T == square, earlier), 1.0, 0.0)
    rank = jnp.sum(same, axis=0, keepdims=True)
    which = lax.broadcasted_iota(jnp.int32, (n, ex), 0).astype(jnp.float32)
    by_owner = jnp.where(which == owner, margin_ref[0:1, :], 0.0)
    place = lax.broadcasted_iota(jnp.int32, (LANES, ex), 0).astype(jnp.float32)
    by_rank = jnp.where(place == rank, 1.0, 0.0)
    ordered = lax.dot_general(
        by_owner, by_rank, NT, precision=lax.Precision.HIGHEST, preferred_element_type=jnp.float32
    )
    sub = lax.broadcasted_iota(jnp.int32, (8, LANES), 0)
    for d in range(n):
        notes[d] = jnp.where(sub == 0, ordered[d : d + 1, :], loss_ref[...])
    me, partner, column, source = seat(n)
    side = me - partner
    deep = n // 2
    others = [lax.rem(me + k, n) for k in range(1, n)]
    greet("rows", others)
    order = list(range(1, deep)) + [0]
    across = {
        k: send_to("rows", partner, grad_ref.at[column[k] - side], crossed.at[k], xsend.at[k], xrecv.at[k])
        for k in order
    }
    told = [
        send_to("rows", peer, notes.at[peer], notes_ref.at[me], nsend.at[k], nrecv.at[k])
        for k, peer in enumerate(others)
    ]
    notes_ref[me] = notes[me]
    along = []
    for k in range(1, deep):
        across[k].wait_recv()
        pair = grad_ref[column[k]].astype(jnp.float32) + crossed[k].astype(jnp.float32)
        paired[k - 1] = pair.astype(jnp.bfloat16)
        along.append(
            send_to("rows", column[k], paired.at[k - 1], held.at[k - 1], send.at[k - 1], recv.at[k - 1])
        )
    across[0].wait_recv()
    total = grad_ref[me].astype(jnp.float32) + crossed[0].astype(jnp.float32)
    for k in range(1, deep):
        along[k - 1].wait_recv()
        total = total + held[k - 1].astype(jnp.float32)
    sum_ref[...] = total
    for k in order:
        across[k].wait_send()
    for copy in along:
        copy.wait_send()
    for copy in told:
        copy.wait()


def on_device(n, nf, tile_values, tile_blocks, tile_counts, labels, owner_rank, weights):
    ex, slots, width = tile_values.shape
    grains = slots // GRAIN
    rows = weights.shape[0]
    deep = n // 2
    f32, i32, bf16 = jnp.float32, jnp.int32, jnp.bfloat16
    shape = jax.ShapeDtypeStruct
    dma = pltpu.SemaphoreType.DMA
    vals = tile_values.reshape(ex * grains, GRAIN, width)

    table = pl.pallas_call(
        functools.partial(gather_kernel, n),
        out_shape=shape((n, rows, width), bf16),
        in_specs=[VM],
        out_specs=VM,
        scratch_shapes=[pltpu.VMEM((rows, width), bf16), dma((deep - 1,)), dma((deep - 1,)), dma((deep,)), dma((deep,))],
        compiler_params=pltpu.CompilerParams(collective_id=0, has_side_effects=True, vmem_limit_bytes=GRANT),
        cost_estimate=COST,
    )(weights).reshape(n * rows, width)

    listed = ex * grains + GROUP
    glist, rlist, nb, idt, partial = pl.pallas_call(
        margin_kernel,
        out_shape=(
            shape((listed,), i32),
            shape((listed,), i32),
            shape((1,), i32),
            shape((ex * grains + 8, LANES), i32),
            shape((8, ex), f32),
        ),
        in_specs=[SM, VM, VM, VM, VM],
        out_specs=(SM, SM, SM, VM, VM),
        scratch_shapes=[pltpu.VMEM((ex * grains + 8, LANES), f32)],
        compiler_params=pltpu.CompilerParams(vmem_limit_bytes=GRANT),
        cost_estimate=COST,
    )(tile_counts.reshape(ex), tile_counts.reshape(1, ex), tile_blocks.T, table, vals)

    margin, resid, loss_part = pl.pallas_call(
        functools.partial(residual_kernel, nf),
        out_shape=(shape((8, ex), f32), shape((1, ex), f32), shape((8, LANES), f32)),
        in_specs=[VM, VM],
        out_specs=(VM, VM, VM),
        scratch_shapes=[pltpu.VMEM((nf, 8, ex), f32), dma((nf - 1,)), dma((nf - 1,))],
        compiler_params=pltpu.CompilerParams(collective_id=1, has_side_effects=True, vmem_limit_bytes=GRANT),
        cost_estimate=COST,
    )(partial, labels.reshape(1, ex))

    grad_part = pl.pallas_call(
        functools.partial(gradient_kernel, grains),
        out_shape=shape((n * rows, width), bf16),
        in_specs=[SM, SM, SM, SM, VM, VM],
        out_specs=VM,
        scratch_shapes=[pltpu.VMEM((n * rows, width), f32)],
        compiler_params=pltpu.CompilerParams(vmem_limit_bytes=GRANT),
        cost_estimate=COST,
    )(glist, rlist, nb, resid, idt, vals)

    gradient, notes = pl.pallas_call(
        functools.partial(scatter_kernel, n),
        out_shape=(shape((rows, width), f32), shape((n, 8, LANES), f32)),
        in_specs=[VM, VM, VM, VM],
        out_specs=(VM, VM),
        scratch_shapes=[
            pltpu.VMEM((n, 8, LANES), f32),
            pltpu.VMEM((deep, rows, width), bf16),
            pltpu.VMEM((deep - 1, rows, width), bf16),
            pltpu.VMEM((deep - 1, rows, width), bf16),
            dma((deep - 1,)),
            dma((deep - 1,)),
            dma((deep,)),
            dma((deep,)),
            dma((n - 1,)),
            dma((n - 1,)),
        ],
        compiler_params=pltpu.CompilerParams(collective_id=2, has_side_effects=True, vmem_limit_bytes=GRANT),
        cost_estimate=COST,
    )(grad_part.reshape(n, rows, width), margin, owner_rank.reshape(1, ex), loss_part)

    owned_margins = notes[:, 0, : ex // n].reshape(ex)
    loss = jnp.sum(notes[:, 1, :]) / (ex * n)
    return owned_margins, gradient, loss


def solution(mesh):
    in_specs = (
        P("rows", "feat", None),
        P("rows", "feat"),
        P("rows", "feat"),
        P("rows"),
        P("rows"),
        P(("feat", "rows"), None),
    )
    out_specs = (P("rows"), P(("feat", "rows"), None), P())
    body = functools.partial(on_device, mesh.shape["rows"], mesh.shape["feat"])
    return jax.shard_map(body, mesh=mesh, in_specs=in_specs, out_specs=out_specs, check_vma=False)
```

profile of v0, /device:TPU:0, one launch (start us, length us, event | category | flops | bytes accessed | tf_op | source)
XLA Modules:
  0.0 69.9 jit_solution(6846787874122256067)
XLA Ops:
  0.6 0.0 copy-start.6
  0.6 0.0 copy-start.2
  0.7 0.9 %copy-done.2 = f32[256,128]{1,0:T(8,128)S(1)} copy-done((f32[256,128]{1,0:T(8,128)S(1)}, f32[256,128]{1,0:T(8,128)}, u32[]{:S(2)}) %copy-start.2) | copy-done | bytes 131096
  1.6 15.6 %shard_map.85 = bf16[8,256,128]{2,1,0:T(8,128)(2,1)S(1)} custom-call(f32[256,128]{1,0:T(8,128)S(1)} %copy-done.2), custom_call_target="tpu_custom_call" | custom-call | bytes 25165824 | tf_op jit(solution)/shard_map/pallas_call | solution.py:274
  17.1 0.0 copy-start
  17.1 2.2 %copy-done = bf16[256,64,128]{2,1,0:T(8,128)(2,1)S(1)} copy-done((bf16[256,64,128]{2,1,0:T(8,128)(2,1)S(1)}, bf16[256,64,128]{2,1,0:T(8,128)(2,1)}, u32[]{:S(2)}) %copy-start) | copy-done | bytes 4194328
  19.3 0.0 copy-start.3
  19.3 0.8 %copy-done.3 = s32[256,64]{0,1:T(8,128)S(1)} copy-done((s32[256,64]{0,1:T(8,128)S(1)}, s32[256,64]{0,1:T(8,128)}, u32[]{:S(2)}) %copy-start.3) | copy-done | bytes 65560
  20.1 0.0 copy-start.4
  20.1 0.7 copy-done.4
  20.8 0.0 copy-start.1
  20.8 0.0 copy-start.5
  20.8 12.1 %shard_map.86 = (s32[1056]{0:T(1024)S(1)}, s32[1056]{0:T(1024)S(1)}, s32[1]{0:T(128)}, s32[1032,128]{1,0:T(8,128)S(1)}, f32[8,256]{1,0:T(8,128)S(1)}) custom-call(s32[256]{0:T(256)S(1)} %bitcast.13, s32[1,256]{1,0:T(1,128)S(1)} %bitcast.14, s32[64,256]{1,0:T(8,128)S(1)} %bitcast.12, bf16[2048,128]{1,0:T(8,128)(2,1)S(1)} %bitcast.10, ...), custom_call_target="tpu_custom_call" | custom-call | bytes 25165824 | tf_op jit(solution)/shard_map/pallas_call | solution.py:285
  32.9 0.0 copy-done.6
  32.9 3.8 %shard_map.87 = (f32[8,256]{1,0:T(8,128)S(1)}, f32[1,256]{1,0:T(1,128)S(1)}, f32[8,128]{1,0:T(8,128)S(1)}) custom-call(f32[8,256]{1,0:T(8,128)S(1)} %get-tuple-element.16.partial_ref, s32[1,256]{1,0:T(1,128)S(1)} %bitcast.16), custom_call_target="tpu_custom_call" | custom-call | bytes 25165824 | tf_op jit(solution)/shard_map/pallas_call | solution.py:301
  36.7 0.0 copy-done.1
  36.7 9.6 %shard_map.88 = bf16[2048,128]{1,0:T(8,128)(2,1)S(1)} custom-call(s32[1056]{0:T(1024)S(1)} %get-tuple-element.13.glist, s32[1056]{0:T(1024)S(1)} %get-tuple-element.14.rlist, s32[1]{0:T(128)} %get-tuple-element.15.nb, f32[1,256]{1,0:T(1,128)S(1)} %get-tuple-element.17.resid, s32[1032,128]{1,0:T(8,128)S(1)} %get-tuple-element.18.idt, ...), custom_call_target="tpu_custom_call" | custom-call | bytes 25165824 | tf_op jit(solution)/shard_map/pallas_call | solution.py:311
  46.3 0.0 copy-done.5
  46.3 19.9 %shard_map.89 = (f32[256,128]{1,0:T(8,128)S(1)}, f32[8,8,128]{2,1,0:T(8,128)S(1)}) custom-call(bf16[8,256,128]{2,1,0:T(8,128)(2,1)S(1)} %bitcast.11, f32[8,256]{1,0:T(8,128)S(1)} %get-tuple-element.19.margin_ref, s32[1,256]{1,0:T(1,128)S(1)} %bitcast.15, f32[8,128]{1,0:T(8,128)S(1)} %get-tuple-element.20.loss_ref), custom_call_target="tpu_custom_call" | custom-call | bytes 25165824 | tf_op jit(solution)/shard_map/pallas_call | solution.py:321
  66.2 0.6 slice_reduce_fusion
  67.5 0.6 reshape_squeeze.3
  68.1 0.7 copy.10
  (1 shorter events, 0.0 us)
Async XLA Ops:
  0.6 32.3 %copy-start.6 = (s32[256]{0:T(256)S(1)}, s32[256]{0:T(256)}, u32[]{:S(2)}) copy-start(s32[256]{0:T(256)} %param.9) | copy-start | bytes 3076
  0.6 0.9 %copy-start.2 = (f32[256,128]{1,0:T(8,128)S(1)}, f32[256,128]{1,0:T(8,128)}, u32[]{:S(2)}) copy-start(f32[256,128]{1,0:T(8,128)} %w_ref.1) | copy-start | bytes 393220
  17.1 2.2 %copy-start = (bf16[256,64,128]{2,1,0:T(8,128)(2,1)S(1)}, bf16[256,64,128]{2,1,0:T(8,128)(2,1)}, u32[]{:S(2)}) copy-start(bf16[256,64,128]{2,1,0:T(8,128)(2,1)} %param.6) | copy-start | bytes 12582916
  19.3 0.8 %copy-start.3 = (s32[256,64]{0,1:T(8,128)S(1)}, s32[256,64]{0,1:T(8,128)}, u32[]{:S(2)}) copy-start(s32[256,64]{0,1:T(8,128)} %param.7) | copy-start | bytes 196612
  20.1 0.7 copy-start.4
  20.8 15.9 %copy-start.1 = (bf16[256,64,128]{2,1,0:T(8,128)(2,1)S(1)}, bf16[256,64,128]{2,1,0:T(8,128)(2,1)}, u32[]{:S(2)}) copy-start(bf16[256,64,128]{2,1,0:T(8,128)(2,1)} %param.6) | copy-start | bytes 12582916
  20.8 25.4 %copy-start.5 = (s32[256]{0:T(256)S(1)}, s32[256]{0:T(256)}, u32[]{:S(2)}) copy-start(s32[256]{0:T(256)} %param.10) | copy-start | bytes 3076
where the time goes:
time: 70.1 us; the launch traced here: 69.9 us
  Pallas kernels  60.8 us (87%)
  local copies, waits for them, and re-layouts  5.93 us (8%)
  between operations  2.51 us (4%)
    pallas_call x1, Pallas kernels, on_device(): pl.pallas_call(functools.partial(scatter_kernel, n), out_shape=(shape((ro...  19.9 us
    pallas_call x1, Pallas kernels, on_device(): pl.pallas_call(functools.partial(gather_kernel, n), out_shape=shape((n, r...  15.6 us
    pallas_call x1, Pallas kernels, on_device(): pl.pallas_call(margin_kernel, out_shape=(shape((listed,), i32), shape((li...  12.1 us
    pallas_call x1, Pallas kernels, on_device(): pl.pallas_call(functools.partial(gradient_kernel, grains), out_shape=shap...  9.57 us
    unnamed x15, local copies, waits for them, and re-layouts  5.27 us
    pallas_call x1, Pallas kernels, on_device(): pl.pallas_call(functools.partial(residual_kernel, nf), out_shape=(shape((...  3.78 us

commit v1 on v0

v1 whole, which is shorter than its diff:
```python
import functools

import jax
import jax.numpy as jnp
from jax import lax
from jax.experimental import pallas as pl
from jax.experimental.pallas import tpu as pltpu
from jax.sharding import PartitionSpec as P

MESH = pl.DeviceIdType.MESH
LANES = 128
GRAIN = 16
GROUP = 32
GRANT = 24 * 1024 * 1024
COST = pl.CostEstimate(flops=0, bytes_accessed=24 * 1024 * 1024, transcendentals=0)
NT = (((1,), (1,)), ((), ()))
NN = (((1,), (0,)), ((), ()))
VM = pl.BlockSpec(memory_space=pltpu.VMEM)
SM = pl.BlockSpec(memory_space=pltpu.SMEM)
ANY = pl.BlockSpec(memory_space=pltpu.HBM)
WIDE = GROUP * GRAIN
PER = LANES // GRAIN


def seat(n):
    me = lax.axis_index("rows")
    side = lax.rem(me, 2)
    partner = me + 1 - 2 * side
    column = [lax.rem(me + 2 * k, n) for k in range(n // 2)]
    source = [lax.rem(me + n - 2 * k, n) for k in range(n // 2)]
    return me, partner, column, source


def call_out(axis, peers):
    barrier = pltpu.get_barrier_semaphore()
    for peer in peers:
        pl.semaphore_signal(barrier, inc=1, device_id={axis: peer}, device_id_type=MESH)
    return lambda: pl.semaphore_wait(barrier, len(peers))


def send_to(axis, peer, source, target, send, recv):
    copy = pltpu.make_async_remote_copy(
        src_ref=source,
        dst_ref=target,
        send_sem=send,
        recv_sem=recv,
        device_id={axis: peer},
        device_id_type=MESH,
    )
    copy.start()
    return copy


def lane_group():
    return lax.broadcasted_iota(jnp.int32, (1, LANES), 1) // GRAIN


def gather_kernel(
    n, w_hbm, ids_hbm, used_hbm, owner_hbm, vals_hbm,
    table_ref, x2_ref, hi_ref, lists_ref, rank_ref, owner_ref,
    w_buf, half, ids, used, own, vals, idt, lists, glist,
    send, recv, xsend, xrecv, here,
):
    local = [
        pltpu.make_async_copy(w_hbm, w_buf, here.at[0]),
        pltpu.make_async_copy(used_hbm, used, here.at[1]),
        pltpu.make_async_copy(ids_hbm, ids, here.at[2]),
        pltpu.make_async_copy(owner_hbm, own, here.at[3]),
        pltpu.make_async_copy(vals_hbm, vals, here.at[4]),
    ]
    for copy in local:
        copy.start()
    me, partner, column, source = seat(n)
    deep = n // 2
    rows = w_buf.shape[0]
    slots, ex = ids.shape
    grains = slots // GRAIN
    joined = call_out("rows", [partner] + column[1:])
    local[0].wait()
    half[...] = w_buf[...].astype(jnp.bfloat16)
    joined()
    across = [send_to("rows", partner, half, table_ref.at[me], xsend.at[0], xrecv.at[0])]
    along = [
        send_to("rows", column[k], half, table_ref.at[me], send.at[k - 1], recv.at[k - 1])
        for k in range(1, deep)
    ]
    table_ref[me] = w_buf[...].astype(jnp.bfloat16)

    f32 = jnp.float32
    local[1].wait()
    count = (used[...] + (GRAIN - 1)) // GRAIN
    sizes = jnp.broadcast_to(count, (LANES, ex)).T
    down = lax.broadcasted_iota(jnp.int32, (ex, LANES), 0)
    ends = sizes
    step = 1
    while step < ex:
        ends = ends + jnp.where(down >= step, pltpu.roll(ends, step, 0), 0)
        step *= 2
    lane = lax.broadcasted_iota(jnp.int32, (1, LANES), 1)
    span = ex * grains // LANES
    for b in range(span):
        place = lane + b * LANES
        past = ends <= place
        which = jnp.sum(jnp.where(past, 1, 0), axis=0, keepdims=True)
        begin = jnp.sum(jnp.where(past, sizes, 0), axis=0, keepdims=True)
        live = which < ex
        q = place - begin
        lists[b : b + 1, :] = jnp.clip(jnp.where(live, which * grains + q, 0), 0, grains * ex - 1)
        lists[span + b : span + b + 1, :] = jnp.clip(jnp.where(live, which + q * ex, grains * ex), 0, grains * ex)
    turns = (ends[ex - 8 : ex, :] + (GROUP - 1)) // GROUP
    lists[2 * span :, :] = jnp.broadcast_to(turns[7:8, :], (8, LANES))
    to_list = pltpu.make_async_copy(lists, glist, here.at[5])
    to_list.start()
    to_next = pltpu.make_async_copy(lists, lists_ref, here.at[6])
    to_next.start()

    local[2].wait()
    live = lax.broadcasted_iota(jnp.int32, (slots, ex), 0) < used[...]
    shifted = jnp.where(live, ids[...] + 1, 0)
    if slots < LANES:
        shifted = jnp.concatenate([shifted, jnp.zeros((LANES - slots, ex), jnp.int32)], axis=0)
    shifted = shifted.T
    spot = lax.broadcasted_iota(jnp.int32, (ex, LANES), 1) // GRAIN
    for q in range(grains):
        piece = jnp.where(spot == q, shifted, 0)
        step = GRAIN
        while step < LANES:
            piece = piece + pltpu.roll(piece, step, 1)
            step *= 2
        idt[q * ex : (q + 1) * ex, :] = piece - 1
    idt[grains * ex :, :] = jnp.full((8, LANES), -1, jnp.int32)

    local[3].wait()
    owner = own[...].astype(f32)
    square = jnp.broadcast_to(owner, (ex, ex))
    earlier = lax.broadcasted_iota(jnp.int32, (ex, ex), 0) < lax.broadcasted_iota(jnp.int32, (ex, ex), 1)
    same = jnp.where(jnp.logical_and(square.T == square, earlier), 1.0, 0.0)
    shift = lax.rem(me * (ex // n), LANES).astype(f32)
    rank = jnp.sum(same, axis=0, keepdims=True) + shift
    spots = lax.broadcasted_iota(jnp.int32, (LANES, ex), 0).astype(f32)
    rank_ref[...] = jnp.where(spots == rank, 1.0, 0.0)
    owner_ref[...] = jnp.broadcast_to(owner, owner_ref.shape)

    to_list.wait()
    to_next.wait()
    local[4].wait()
    group = lane_group()
    tall = x2_ref.shape[1] // 2

    def prepare(t, carry):
        row = t * GROUP // LANES
        col = lax.rem(t * GROUP, LANES)
        values = jnp.concatenate([vals[glist[row, col + i]] for i in range(GROUP)], axis=0)
        parts = []
        for h in range(GROUP // PER):
            line = idt[pl.ds(glist[span + row, col + h * PER], 1), :]
            for i in range(1, PER):
                line = jnp.where(group == i, idt[pl.ds(glist[span + row, col + h * PER + i], 1), :], line)
            parts.append(line)
        id_row = jnp.concatenate(parts, axis=1)
        chunk = id_row // rows
        odd = lax.rem(chunk, 2)
        high = jnp.where(id_row < 0, -1, (chunk // 2) * rows + lax.rem(id_row, rows))
        hi_ref[t] = high
        odd = jnp.broadcast_to(odd.astype(f32), (16, WIDE))
        odd_half = jnp.concatenate([odd.astype(jnp.bfloat16)] * (tall // 16), axis=0)
        even_half = jnp.concatenate([(1.0 - odd).astype(jnp.bfloat16)] * (tall // 16), axis=0)
        flipped = values.T
        x2_ref[t, 0:tall, :] = flipped * even_half
        x2_ref[t, tall:, :] = flipped * odd_half
        return carry

    total = x2_ref.shape[0]
    for k in range(deep):
        if k > 0:
            along[k - 1].wait_recv()
            block = table_ref.at[source[k]]
            across.append(send_to("rows", partner, block, block, xsend.at[k], xrecv.at[k]))
        lax.fori_loop(total * k // deep, total * (k + 1) // deep, prepare, jnp.int32(0))
    for copy in along:
        copy.wait_send()
    for copy in across:
        copy.wait()


def margin_kernel(lists, table_ref, x2_ref, hi_ref, partial_ref, terms):
    n, rows, _ = table_ref.shape
    ex = partial_ref.shape[1]
    grains = terms.shape[0] // ex
    span = ex * grains // LANES
    terms[...] = jnp.zeros_like(terms)
    group = lane_group()

    def turn(t, carry):
        x2 = x2_ref[t]
        offset = jnp.broadcast_to(hi_ref[t], (8, WIDE)) - lax.broadcasted_iota(jnp.int32, (8, WIDE), 0)
        found = jnp.zeros((8, WIDE), jnp.float32)
        for k in range(n // 2):
            pair = jnp.concatenate([table_ref[2 * k], table_ref[2 * k + 1]], axis=1)
            scores = lax.dot_general(pair, x2, NN, preferred_element_type=jnp.float32)
            for i in range(rows // 8):
                found = jnp.where(offset == k * rows + i * 8, scores[i * 8 : i * 8 + 8, :], found)
        term = jnp.sum(found, axis=0, keepdims=True)
        row = t * GROUP // LANES
        col = lax.rem(t * GROUP, LANES)
        for i in range(GROUP):
            h = i // PER
            mine = jnp.where(group == i % PER, term[:, h * LANES : (h + 1) * LANES], 0.0)
            terms[pl.ds(lists[span + row, col + i], 1), :] = mine
        return carry

    lax.fori_loop(0, lists[2 * span, 0], turn, jnp.int32(0))
    spread = terms[0:ex, :]
    for q in range(1, grains):
        spread = spread + terms[q * ex : (q + 1) * ex, :]
    partial_ref[...] = jnp.broadcast_to(jnp.sum(spread.T, axis=0, keepdims=True), partial_ref.shape)


def residual_kernel(n, partial_ref, labels_ref, margin_ref, resid_ref, loss_ref, held, send, recv):
    me = lax.axis_index("feat")
    peers = [lax.rem(me + k, n) for k in range(1, n)]
    call_out("feat", peers)()
    copies = [
        send_to("feat", peer, partial_ref, held.at[me], send.at[k], recv.at[k])
        for k, peer in enumerate(peers)
    ]
    held[me] = partial_ref[...]
    for copy in copies:
        copy.wait()
    margin = held[0]
    for k in range(1, n):
        margin = margin + held[k]
    label = labels_ref[...].astype(jnp.float32)
    residual = 1.0 / (1.0 + jnp.exp(-margin)) - label
    margin_ref[...] = margin
    resid_ref[...] = residual.astype(jnp.bfloat16).astype(jnp.float32)[0:1, :]
    term = jnp.maximum(margin, 0.0) + jnp.log1p(jnp.exp(-jnp.abs(margin))) - label * margin
    total = term[:, 0:LANES]
    for h in range(1, term.shape[1] // LANES):
        total = total + term[:, h * LANES : (h + 1) * LANES]
    loss_ref[...] = total


def gradient_kernel(grains, lists, resid, x2_ref, hi_ref, out_ref, total):
    total[...] = jnp.zeros_like(total)
    n, rows, width = out_ref.shape
    span = resid.shape[1] * grains // LANES
    group = lane_group()

    def turn(t, carry):
        x2 = x2_ref[t]
        offset = jnp.broadcast_to(hi_ref[t], (8, WIDE)) - lax.broadcasted_iota(jnp.int32, (8, WIDE), 0)
        row_at = t * GROUP // LANES
        col = lax.rem(t * GROUP, LANES)
        parts = []
        for h in range(GROUP // PER):
            row = jnp.zeros((1, LANES), jnp.float32)
            for i in range(PER):
                row = jnp.where(group == i, resid[0, lists[row_at, col + h * PER + i] // grains], row)
            parts.append(row)
        factor = jnp.broadcast_to(jnp.concatenate(parts, axis=1), (8, WIDE))
        for k in range(n // 2):
            spread = jnp.concatenate(
                [jnp.where(offset == k * rows + i * 8, factor, 0.0) for i in range(rows // 8)], axis=0
            ).astype(jnp.bfloat16)
            total[k * rows : (k + 1) * rows, :] += lax.dot_general(
                spread, x2, NT, preferred_element_type=jnp.float32
            )
        return carry

    lax.fori_loop(0, lists[2 * span, 0], turn, jnp.int32(0))
    for k in range(n // 2):
        out_ref[2 * k] = total[k * rows : (k + 1) * rows, 0:width].astype(jnp.bfloat16)
        out_ref[2 * k + 1] = total[k * rows : (k + 1) * rows, width:].astype(jnp.bfloat16)


def scatter_kernel(
    n, grad_ref, margin_ref, owner_ref, rank_ref, loss_ref,
    sum_ref, notes_ref, notes, crossed, paired, held, send, recv, xsend, xrecv, nsend, nrecv,
):
    ex = margin_ref.shape[1]
    me, partner, column, source = seat(n)
    side = me - partner
    deep = n // 2
    others = [lax.rem(me + k, n) for k in range(1, n)]
    joined = call_out("rows", others)
    which = lax.broadcasted_iota(jnp.int32, (n, ex), 0).astype(jnp.float32)
    by_owner = jnp.where(which == owner_ref[0:1, :], margin_ref[0:1, :], 0.0)
    ordered = lax.dot_general(
        by_owner, rank_ref[...], NT, precision=lax.Precision.HIGHEST, preferred_element_type=jnp.float32
    )
    sub = lax.broadcasted_iota(jnp.int32, (8, LANES), 0)
    for d in range(n):
        notes[d] = jnp.where(sub == 0, ordered[d : d + 1, :], loss_ref[...])
    joined()
    order = list(range(1, deep)) + [0]
    across = {
        k: send_to("rows", partner, grad_ref.at[column[k] - side], crossed.at[k], xsend.at[k], xrecv.at[k])
        for k in order
    }
    told = [
        send_to("rows", peer, notes.at[peer], notes_ref.at[me], nsend.at[k], nrecv.at[k])
        for k, peer in enumerate(others)
    ]
    notes_ref[me] = notes[me]
    along = []
    for k in range(1, deep):
        across[k].wait_recv()
        pair = grad_ref[column[k]].astype(jnp.float32) + crossed[k].astype(jnp.float32)
        paired[k - 1] = pair.astype(jnp.bfloat16)
        along.append(
            send_to("rows", column[k], paired.at[k - 1], held.at[k - 1], send.at[k - 1], recv.at[k - 1])
        )
    across[0].wait_recv()
    total = grad_ref[me].astype(jnp.float32) + crossed[0].astype(jnp.float32)
    for k in range(1, deep):
        along[k - 1].wait_recv()
        total = total + held[k - 1].astype(jnp.float32)
    sum_ref[...] = total
    for k in order:
        across[k].wait_send()
    for copy in along:
        copy.wait_send()
    for copy in told:
        copy.wait()


def finish_kernel(sum_ref, notes_ref, owned_ref, grad_ref, loss_ref):
    n = notes_ref.shape[0]
    ex = owned_ref.shape[1]
    grad_ref[...] = sum_ref[...]
    for h in range(ex // LANES):
        row = jnp.zeros((1, LANES), jnp.float32)
        for d in range(n):
            if d * (ex // n) // LANES == h:
                row = row + notes_ref[d, 0:1, :]
        owned_ref[:, h * LANES : (h + 1) * LANES] = row
    loss = jnp.zeros((1, LANES), jnp.float32)
    for d in range(n):
        loss = loss + notes_ref[d, 1:2, :]
    loss_ref[0, 0] = jnp.sum(loss) * (1.0 / (ex * n))


def on_device(n, nf, tile_values, tile_blocks, tile_counts, labels, owner_rank, weights):
    ex, slots, width = tile_values.shape
    grains = slots // GRAIN
    rows = weights.shape[0]
    deep = n // 2
    turns = ex * grains // GROUP
    span = ex * grains // LANES
    f32, i32, bf16 = jnp.float32, jnp.int32, jnp.bfloat16
    shape = jax.ShapeDtypeStruct
    dma = pltpu.SemaphoreType.DMA
    vals = tile_values.reshape(ex * grains, GRAIN, width)

    table, x2, high, lists, rank, owner = pl.pallas_call(
        functools.partial(gather_kernel, n),
        out_shape=(
            shape((n, rows, width), bf16),
            shape((turns, 2 * width, WIDE), bf16),
            shape((turns, 1, WIDE), i32),
            shape((2 * span + 8, LANES), i32),
            shape((LANES, ex), f32),
            shape((8, ex), f32),
        ),
        in_specs=[ANY] * 5,
        out_specs=(VM, VM, VM, SM, VM, VM),
        scratch_shapes=[
            pltpu.VMEM((rows, width), f32),
            pltpu.VMEM((rows, width), bf16),
            pltpu.VMEM((slots, ex), i32),
            pltpu.VMEM((1, ex), i32),
            pltpu.VMEM((1, ex), i32),
            pltpu.VMEM((ex * grains, GRAIN, width), bf16),
            pltpu.VMEM((ex * grains + 8, LANES), i32),
            pltpu.VMEM((2 * span + 8, LANES), i32),
            pltpu.SMEM((2 * span + 8, LANES), i32),
            dma((deep - 1,)), dma((deep - 1,)), dma((deep,)), dma((deep,)), dma((7,)),
        ],
        compiler_params=pltpu.CompilerParams(collective_id=0, has_side_effects=True, vmem_limit_bytes=GRANT),
        cost_estimate=COST,
    )(*[
        pltpu.with_memory_space_constraint(a, pltpu.HBM)
        for a in (weights, tile_blocks.T, tile_counts.reshape(1, ex), owner_rank.reshape(1, ex), vals)
    ])

    partial = pl.pallas_call(
        margin_kernel,
        out_shape=shape((8, ex), f32),
        in_specs=[SM, VM, VM, VM],
        out_specs=VM,
        scratch_shapes=[pltpu.VMEM((ex * grains + 8, LANES), f32)],
        compiler_params=pltpu.CompilerParams(vmem_limit_bytes=GRANT),
        cost_estimate=COST,
    )(lists, table, x2, high)

    margin, resid, loss_part = pl.pallas_call(
        functools.partial(residual_kernel, nf),
        out_shape=(shape((8, ex), f32), shape((1, ex), f32), shape((8, LANES), f32)),
        in_specs=[VM, VM],
        out_specs=(VM, VM, VM),
        scratch_shapes=[pltpu.VMEM((nf, 8, ex), f32), dma((nf - 1,)), dma((nf - 1,))],
        compiler_params=pltpu.CompilerParams(collective_id=1, has_side_effects=True, vmem_limit_bytes=GRANT),
        cost_estimate=COST,
    )(partial, labels.reshape(1, ex))

    grad_part = pl.pallas_call(
        functools.partial(gradient_kernel, grains),
        out_shape=shape((n, rows, width), bf16),
        in_specs=[SM, SM, VM, VM],
        out_specs=VM,
        scratch_shapes=[pltpu.VMEM((deep * rows, 2 * width), f32)],
        compiler_params=pltpu.CompilerParams(vmem_limit_bytes=GRANT),
        cost_estimate=COST,
    )(lists, resid, x2, high)

    total, notes = pl.pallas_call(
        functools.partial(scatter_kernel, n),
        out_shape=(shape((rows, width), f32), shape((n, 8, LANES), f32)),
        in_specs=[VM] * 5,
        out_specs=(VM, VM),
        scratch_shapes=[
            pltpu.VMEM((n, 8, LANES), f32),
            pltpu.VMEM((deep, rows, width), bf16),
            pltpu.VMEM((deep - 1, rows, width), bf16),
            pltpu.VMEM((deep - 1, rows, width), bf16),
            dma((deep - 1,)),
            dma((deep - 1,)),
            dma((deep,)),
            dma((deep,)),
            dma((n - 1,)),
            dma((n - 1,)),
        ],
        compiler_params=pltpu.CompilerParams(collective_id=2, has_side_effects=True, vmem_limit_bytes=GRANT),
        cost_estimate=COST,
    )(grad_part, margin, owner, rank, loss_part)

    owned, gradient, loss = pl.pallas_call(
        finish_kernel,
        out_shape=(shape((1, ex), f32), shape((rows, width), f32), shape((1, 1), f32)),
        in_specs=[VM, VM],
        out_specs=(VM, VM, SM),
        compiler_params=pltpu.CompilerParams(vmem_limit_bytes=GRANT),
        cost_estimate=COST,
    )(total, notes)
    return owned.reshape(ex), gradient, loss.reshape(())


def solution(mesh):
    in_specs = (
        P("rows", "feat", None),
        P("rows", "feat"),
        P("rows", "feat"),
        P("rows"),
        P("rows"),
        P(("feat", "rows"), None),
    )
    out_specs = (P("rows"), P(("feat", "rows"), None), P())
    body = functools.partial(on_device, mesh.shape["rows"], mesh.shape["feat"])
    return jax.shard_map(body, mesh=mesh, in_specs=in_specs, out_specs=out_specs, check_vma=False)
```

time: 70.1 us -> 50.8 us (0.72)
  Pallas kernels: 60.8 us -> 49.7 us
  local copies, waits for them, and re-layouts: 5.93 us -> 0.01 us
  between operations: 2.51 us -> 0.69 us
    unnamed x15 -> x2, local copies, waits for them, and re-layouts: 5.27 us -> 0.01 us
    pallas_call x2 -> x3, Pallas kernels: 27.6 us -> 22.9 us  [the longest x1 17.2 us: on_device(): pl.pallas_call(functools.partial(gather_kernel, n), out_shape=(shape((n,...]
    pallas_call x1, Pallas kernels: 9.57 us -> 5.87 us  [on_device(): pl.pallas_call(functools.partial(gradient_kernel, grains), out_shape=shap...]
    pallas_call x1, Pallas kernels: 19.9 us -> 17.1 us  [on_device(): pl.pallas_call(functools.partial(scatter_kernel, n), out_shape=(shape((ro...]
where the time goes in v1:
time: 50.8 us; the launch traced here: 50.4 us
  Pallas kernels  49.7 us (98%)
  between operations  0.69 us (1%)
    pallas_call x1, Pallas kernels, on_device(): pl.pallas_call(functools.partial(gather_kernel, n), out_shape=(shape((n,...  17.2 us
    pallas_call x1, Pallas kernels, on_device(): pl.pallas_call(functools.partial(scatter_kernel, n), out_shape=(shape((ro...  17.1 us
    pallas_call x1, Pallas kernels, on_device(): pl.pallas_call(functools.partial(gradient_kernel, grains), out_shape=shap...  5.87 us
    pallas_call x1, Pallas kernels, on_device(): pl.pallas_call(margin_kernel, out_shape=shape((8, ex), f32), in_specs=[SM...  5.07 us
    pallas_call x1, Pallas kernels, on_device(): pl.pallas_call(functools.partial(residual_kernel, nf), out_shape=(shape((...  3.78 us

profile of v1, /device:TPU:0, one launch (start us, length us, event | category | flops | bytes accessed | tf_op | source)
XLA Modules:
  0.0 50.4 jit_solution(3112576677730910936)
XLA Ops:
  0.6 0.0 copy-start
  0.6 17.2 %shard_map.85 = (bf16[8,256,128]{2,1,0:T(8,128)(2,1)S(1)}, bf16[32,256,512]{2,1,0:T(8,128)(2,1)S(1)}, s32[32,1,512]{2,1,0:T(1,128)S(1)}, s32[24,128]{1,0:T(8,128...) custom-call(f32[256,128]{1,0:T(8,128)} %w_hbm.1, s32[64,256]{1,0:T(8,128)} %bitcast.9, s32[1,256]{1,0:T(1,128)} %bitcast.10, ...), custom_call_target="tpu_custom_call" | custom-call | bytes 25165824 | tf_op jit(solution)/shard_map/pallas_call | solution.py:356
  17.8 5.1 %shard_map.86.partial_ref = f32[8,256]{1,0:T(8,128)S(1)} custom-call(s32[24,128]{1,0:T(8,128)S(1)} %get-tuple-element.17.lists, bf16[8,256,128]{2,1,0:T(8,128)(2,1)S(1)} %get-tuple-element.18.table_ref, bf16[32,256,512]{2,1,0:T(8,128)(2,1)S(1)} %get-tuple-element.19.x2_ref, s32[32,1,512]{2,1,0:T(1,128)S(1)} %get-tuple-element.20.hi_ref), custom_call_target="tpu_custom_call" | custom-call | bytes 25165824 | tf_op jit(solution)/shard_map/pallas_call | solution.py:387
  22.9 0.0 copy-done
  22.9 3.8 %shard_map.87 = (f32[8,256]{1,0:T(8,128)S(1)}, f32[1,256]{1,0:T(1,128)S(1)}, f32[8,128]{1,0:T(8,128)S(1)}) custom-call(f32[8,256]{1,0:T(8,128)S(1)} %shard_map.86.partial_ref, s32[1,256]{1,0:T(1,128)S(1)} %bitcast.7), custom_call_target="tpu_custom_call" | custom-call | bytes 25165824 | tf_op jit(solution)/shard_map/pallas_call | solution.py:397
  26.7 5.9 %shard_map.88.grad_ref = bf16[8,256,128]{2,1,0:T(8,128)(2,1)S(1)} custom-call(s32[24,128]{1,0:T(8,128)S(1)} %get-tuple-element.17.lists, f32[1,256]{1,0:T(1,128)S(1)} %get-tuple-element.21.resid, bf16[32,256,512]{2,1,0:T(8,128)(2,1)S(1)} %get-tuple-element.19.x2_ref, s32[32,1,512]{2,1,0:T(1,128)S(1)} %get-tuple-element.20.hi_ref), custom_call_target="tpu_custom_call" | custom-call | bytes 25165824 | tf_op jit(solution)/shard_map/pallas_call | solution.py:407
  32.6 17.1 %shard_map.89 = (f32[256,128]{1,0:T(8,128)S(1)}, f32[8,8,128]{2,1,0:T(8,128)S(1)}) custom-call(bf16[8,256,128]{2,1,0:T(8,128)(2,1)S(1)} %shard_map.88.grad_ref, f32[8,256]{1,0:T(8,128)S(1)} %get-tuple-element.22.margin_ref, f32[8,256]{1,0:T(8,128)S(1)} %get-tuple-element.23.owner_ref, f32[128,256]{1,0:T(8,128)S(1)} %get-tuple-element.24.rank_ref, ...), custom_call_target="tpu_custom_call" | custom-call | bytes 25165824 | tf_op jit(solution)/shard_map/pallas_call | solution.py:417
  49.7 0.7 %shard_map.90 = (f32[1,256]{1,0:T(1,128)}, f32[256,128]{1,0:T(8,128)}, f32[1,1]{1,0:T(1,128)}) custom-call(f32[256,128]{1,0:T(8,128)S(1)} %get-tuple-element.26.sum_ref, f32[8,8,128]{2,1,0:T(8,128)S(1)} %get-tuple-element.27.notes_ref), custom_call_target="tpu_custom_call" | custom-call | bytes 25165824 | tf_op jit(solution)/shard_map/pallas_call | solution.py:438
Async XLA Ops:
  0.6 22.3 %copy-start = (s32[256]{0:T(256)S(1)}, s32[256]{0:T(256)}, u32[]{:S(2)}) copy-start(s32[256]{0:T(256)} %param.9) | copy-start | bytes 3076

commit v2 on v1

v2 whole, which is shorter than its diff:
```python
import functools

import jax
import jax.numpy as jnp
from jax import lax
from jax.experimental import pallas as pl
from jax.experimental.pallas import tpu as pltpu
from jax.sharding import PartitionSpec as P

MESH = pl.DeviceIdType.MESH
LANES = 128
GRAIN = 16
GROUP = 32
GRANT = 24 * 1024 * 1024
COST = pl.CostEstimate(flops=0, bytes_accessed=24 * 1024 * 1024, transcendentals=0)
NT = (((1,), (1,)), ((), ()))
NN = (((1,), (0,)), ((), ()))
VM = pl.BlockSpec(memory_space=pltpu.VMEM)
SM = pl.BlockSpec(memory_space=pltpu.SMEM)
ANY = pl.BlockSpec(memory_space=pltpu.HBM)
WIDE = GROUP * GRAIN
PER = LANES // GRAIN
CUT = 256


def seat(n):
    me = lax.axis_index("rows")
    side = lax.rem(me, 2)
    spot = me // 2
    partner = me + 1 - 2 * side
    deep = n // 2
    tables = [sorted((z for z in range(deep) if z != at), key=lambda z: -abs(z - at)) for at in range(deep)]
    far = []
    for j in range(deep - 1):
        pick = tables[0][j]
        for at in range(1, deep):
            pick = pick + (tables[at][j] - tables[at - 1][j]) * ((spot + deep - at) // deep)
        far.append(pick)
    return me, side, spot, partner, far


def call_out(axis, peers):
    barrier = pltpu.get_barrier_semaphore()
    for peer in peers:
        pl.semaphore_signal(barrier, inc=1, device_id={axis: peer}, device_id_type=MESH)
    return lambda: pl.semaphore_wait(barrier, len(peers))


def copy_to(axis, peer, source, target, send, recv):
    return pltpu.make_async_remote_copy(
        src_ref=source,
        dst_ref=target,
        send_sem=send,
        recv_sem=recv,
        device_id={axis: peer},
        device_id_type=MESH,
    )


def send_to(*args):
    copy = copy_to(*args)
    copy.start()
    return copy


def lane_group():
    return lax.broadcasted_iota(jnp.int32, (1, LANES), 1) // GRAIN


def own_lanes():
    sub = lax.broadcasted_iota(jnp.int32, (8, LANES), 0)
    return sub == lax.broadcasted_iota(jnp.int32, (8, LANES), 1) // GRAIN


def offsets(row):
    return jnp.broadcast_to(row, (8, WIDE)) - lax.broadcasted_iota(jnp.int32, (8, WIDE), 0)


def select_scores(pair, x2, offset, first, found):
    scores = lax.dot_general(pair, x2, NN, preferred_element_type=jnp.float32)
    for i in range(pair.shape[0] // 8):
        found = jnp.where(offset == first + i * 8, scores[i * 8 : i * 8 + 8, :], found)
    return found


def spread_sum(x2, offset, factor, first, rows):
    spread = jnp.concatenate(
        [jnp.where(offset == first + i * 8, factor, 0.0) for i in range(rows // 8)], axis=0
    ).astype(jnp.bfloat16)
    return lax.dot_general(spread, x2, NT, preferred_element_type=jnp.float32)


def gather_kernel(
    n, w_hbm, ids_hbm, used_hbm, owner_hbm, vals_hbm,
    table_ref, x2_ref, hi_ref, lists_ref, rank_ref, owner_ref, first_ref,
    w_buf, half, ids, used, own, vals, idt, lists, glist, found,
    send, recv, xsend, xrecv, here,
):
    local = [
        pltpu.make_async_copy(w_hbm, w_buf, here.at[0]),
        pltpu.make_async_copy(used_hbm, used, here.at[1]),
        pltpu.make_async_copy(ids_hbm, ids, here.at[2]),
        pltpu.make_async_copy(owner_hbm, own, here.at[3]),
        pltpu.make_async_copy(vals_hbm, vals, here.at[4]),
    ]
    for copy in local:
        copy.start()
    me, side, spot, partner, far = seat(n)
    deep = n // 2
    rows = w_buf.shape[0]
    slots, ex = ids.shape
    grains = slots // GRAIN
    joined = call_out("rows", [partner] + [2 * z + side for z in far])
    local[0].wait()
    half[...] = w_buf[...].astype(jnp.bfloat16)
    joined()
    across = [send_to("rows", partner, half, table_ref.at[me], xsend.at[spot], xrecv.at[spot])]
    along = [
        send_to("rows", 2 * z + side, half, table_ref.at[me], send.at[j], recv.at[spot])
        for j, z in enumerate(far)
    ]
    table_ref[me] = w_buf[...].astype(jnp.bfloat16)

    f32 = jnp.float32
    local[1].wait()
    count = (used[...] + (GRAIN - 1)) // GRAIN - 1
    sizes = jnp.broadcast_to(count, (LANES, ex)).T
    down = lax.broadcasted_iota(jnp.int32, (ex, LANES), 0)
    ends = sizes
    step = 1
    while step < ex:
        ends = ends + jnp.where(down >= step, pltpu.roll(ends, step, 0), 0)
        step *= 2
    lane = lax.broadcasted_iota(jnp.int32, (1, LANES), 1)
    span = ex * (grains - 1) // LANES
    hold = lists.shape[0] // 3
    for b in range(span):
        place = lane + b * LANES
        past = ends <= place
        which = jnp.sum(jnp.where(past, 1, 0), axis=0, keepdims=True)
        begin = jnp.sum(jnp.where(past, sizes, 0), axis=0, keepdims=True)
        live = which < ex
        q = place - begin + 1
        lists[b : b + 1, :] = jnp.clip(jnp.where(live, which * grains + q, 0), 0, grains * ex - 1)
        lists[hold + b : hold + b + 1, :] = jnp.clip(jnp.where(live, which + q * ex, grains * ex), 0, grains * ex)
    turns = (ends[ex - 8 : ex, :] + (GROUP - 1)) // GROUP
    lists[2 * hold :, :] = jnp.broadcast_to(turns[7:8, :], (hold, LANES))
    to_list = pltpu.make_async_copy(lists, glist, here.at[5])
    to_list.start()
    to_next = pltpu.make_async_copy(lists, lists_ref, here.at[6])
    to_next.start()

    local[2].wait()
    live = lax.broadcasted_iota(jnp.int32, (slots, ex), 0) < used[...]
    shifted = jnp.where(live, ids[...] + 1, 0)
    if slots < LANES:
        shifted = jnp.concatenate([shifted, jnp.zeros((LANES - slots, ex), jnp.int32)], axis=0)
    shifted = shifted.T
    grain_of = lax.broadcasted_iota(jnp.int32, (ex, LANES), 1) // GRAIN
    for q in range(grains):
        piece = jnp.where(grain_of == q, shifted, 0)
        step = GRAIN
        while step < LANES:
            piece = piece + pltpu.roll(piece, step, 1)
            step *= 2
        idt[q * ex : (q + 1) * ex, :] = piece - 1
    idt[grains * ex :, :] = jnp.full((8, LANES), -1, jnp.int32)

    tall = x2_ref.shape[1] // 2

    def put(t, values, id_row):
        chunk = id_row // rows
        odd = lax.rem(chunk, 2)
        high = jnp.where(id_row < 0, -1, (chunk // 2) * rows + lax.rem(id_row, rows))
        hi_ref[t] = high
        odd = jnp.broadcast_to(odd.astype(f32), (16, WIDE))
        odd_half = jnp.concatenate([odd.astype(jnp.bfloat16)] * (tall // 16), axis=0)
        even_half = jnp.concatenate([(1.0 - odd).astype(jnp.bfloat16)] * (tall // 16), axis=0)
        flipped = values.T
        x2_ref[t, 0:tall, :] = flipped * even_half
        x2_ref[t, tall:, :] = flipped * odd_half

    mine = own_lanes()
    group = lane_group()
    steady = ex // GROUP

    def prepare_first(t, carry):
        at = t * GROUP
        values = jnp.concatenate([vals[(at + i) * grains] for i in range(GROUP)], axis=0)
        parts = [
            jnp.sum(jnp.where(mine, idt[pl.ds(at + h * PER, PER), :], 0), axis=0, keepdims=True)
            for h in range(GROUP // PER)
        ]
        put(t, values, jnp.concatenate(parts, axis=1))
        found[t] = jnp.zeros((8, WIDE), f32)
        return carry

    def prepare_rest(t, carry):
        row = t * GROUP // LANES
        col = lax.rem(t * GROUP, LANES)
        values = jnp.concatenate([vals[glist[row, col + i]] for i in range(GROUP)], axis=0)
        parts = []
        for h in range(GROUP // PER):
            line = idt[pl.ds(glist[hold + row, col + h * PER], 1), :]
            for i in range(1, PER):
                line = jnp.where(group == i, idt[pl.ds(glist[hold + row, col + h * PER + i], 1), :], line)
            parts.append(line)
        put(steady + t, values, jnp.concatenate(parts, axis=1))
        return carry

    def score(z):
        pair = jnp.concatenate([table_ref[2 * z], table_ref[2 * z + 1]], axis=1)

        def turn(t, carry):
            found[t] = select_scores(pair, x2_ref[t], offsets(hi_ref[t]), z * rows, found[t])
            return carry

        lax.fori_loop(0, steady, turn, jnp.int32(0), unroll=2)

    local[4].wait()
    lax.fori_loop(0, steady, prepare_first, jnp.int32(0), unroll=2)
    to_list.wait()
    to_next.wait()

    def arrival(z):
        return copy_to("rows", partner, half, table_ref.at[2 * z + side], send.at[0], recv.at[z])

    def crossing(z):
        return copy_to("rows", partner, half, table_ref.at[2 * z + 1 - side], send.at[0], xrecv.at[z])

    near = far[::-1]
    total = x2_ref.shape[0] - steady
    cuts = [total * j // (deep - 1) for j in range(deep)]
    cuts = [c // 2 * 2 for c in cuts[:-1]] + [total]
    for j, z in enumerate(near):
        arrival(z).wait_recv()
        block = table_ref.at[2 * z + side]
        across.append(send_to("rows", partner, block, block, xsend.at[z], xrecv.at[z]))
        lax.fori_loop(cuts[j], cuts[j + 1], prepare_rest, jnp.int32(0), unroll=2 if deep == 4 else 1)
        done = spot if j == 0 else near[j - 1]
        crossing(done).wait_recv()
        score(done)

    local[3].wait()
    owner = own[...].astype(f32)
    square = jnp.broadcast_to(owner, (ex, ex))
    earlier = lax.broadcasted_iota(jnp.int32, (ex, ex), 0) < lax.broadcasted_iota(jnp.int32, (ex, ex), 1)
    same = jnp.where(jnp.logical_and(square.T == square, earlier), 1.0, 0.0)
    shift = lax.rem(me * (ex // n), LANES).astype(f32)
    rank = jnp.sum(same, axis=0, keepdims=True) + shift
    places = lax.broadcasted_iota(jnp.int32, (LANES, ex), 0).astype(f32)
    rank_ref[...] = jnp.where(places == rank, 1.0, 0.0)
    owner_ref[...] = jnp.broadcast_to(owner, owner_ref.shape)

    crossing(near[-1]).wait_recv()
    score(near[-1])
    for t in range(steady):
        term = jnp.sum(found[t], axis=0, keepdims=True)
        for h in range(GROUP // PER):
            at = t * GROUP + h * PER
            first_ref[at : at + PER, :] = jnp.where(mine, term[:, h * LANES : (h + 1) * LANES], 0.0)
    for copy in along:
        copy.wait_send()
    for copy in across:
        copy.wait_send()


def margin_kernel(lists, table_ref, x2_ref, hi_ref, first_ref, partial_ref, terms):
    n, rows, _ = table_ref.shape
    ex = partial_ref.shape[1]
    grains = terms.shape[0] // ex
    hold = lists.shape[0] // 3
    steady = ex // GROUP
    terms[ex:, :] = jnp.zeros((terms.shape[0] - ex, LANES), jnp.float32)
    group = lane_group()

    def one(t):
        x2 = x2_ref[steady + t]
        offset = offsets(hi_ref[steady + t])
        found = jnp.zeros((8, WIDE), jnp.float32)
        for k in range(n // 2):
            pair = jnp.concatenate([table_ref[2 * k], table_ref[2 * k + 1]], axis=1)
            found = select_scores(pair, x2, offset, k * rows, found)
        return jnp.sum(found, axis=0, keepdims=True)

    def keep(t, term):
        row = t * GROUP // LANES
        col = lax.rem(t * GROUP, LANES)
        for i in range(GROUP):
            h = i // PER
            mine = jnp.where(group == i % PER, term[:, h * LANES : (h + 1) * LANES], 0.0)
            terms[pl.ds(lists[hold + row, col + i], 1), :] = mine

    def turn(t, carry):
        a = one(2 * t)
        b = one(2 * t + 1)
        keep(2 * t, a)
        keep(2 * t + 1, b)
        return carry

    lax.fori_loop(0, (lists[2 * hold, 0] + 1) // 2, turn, jnp.int32(0))
    spread = first_ref[...]
    for q in range(1, grains):
        spread = spread + terms[q * ex : (q + 1) * ex, :]
    partial_ref[...] = jnp.broadcast_to(jnp.sum(spread.T, axis=0, keepdims=True), partial_ref.shape)


def residual_kernel(n, partial_ref, labels_ref, margin_ref, resid_ref, loss_ref, held, send, recv):
    me = lax.axis_index("feat")
    peers = [lax.rem(me + k, n) for k in range(1, n)]
    call_out("feat", peers)()
    copies = [
        send_to("feat", peer, partial_ref, held.at[me], send.at[k], recv.at[k])
        for k, peer in enumerate(peers)
    ]
    held[me] = partial_ref[...]
    for copy in copies:
        copy.wait()
    margin = held[0]
    for k in range(1, n):
        margin = margin + held[k]
    label = labels_ref[...].astype(jnp.float32)
    residual = 1.0 / (1.0 + jnp.exp(-margin)) - label
    margin_ref[...] = margin
    resid_ref[...] = residual.astype(jnp.bfloat16).astype(jnp.float32)[0:1, :]
    term = jnp.maximum(margin, 0.0) + jnp.log1p(jnp.exp(-jnp.abs(margin))) - label * margin
    total = term[:, 0:LANES]
    for h in range(1, term.shape[1] // LANES):
        total = total + term[:, h * LANES : (h + 1) * LANES]
    loss_ref[...] = total


def rest_kernel(grains, lists, resid, x2_ref, hi_ref, total):
    total[...] = jnp.zeros_like(total)
    hold = lists.shape[0] // 3
    rows = CUT
    steady = resid.shape[1] // GROUP
    group = lane_group()

    def turn(t, carry):
        x2 = x2_ref[steady + t]
        offset = offsets(hi_ref[steady + t])
        row_at = t * GROUP // LANES
        col = lax.rem(t * GROUP, LANES)
        parts = []
        for h in range(GROUP // PER):
            row = jnp.zeros((1, LANES), jnp.float32)
            for i in range(PER):
                row = jnp.where(group == i, resid[0, lists[row_at, col + h * PER + i] // grains], row)
            parts.append(row)
        factor = jnp.broadcast_to(jnp.concatenate(parts, axis=1), (8, WIDE))
        for k in range(total.shape[0] // rows):
            total[k * rows : (k + 1) * rows, :] += spread_sum(x2, offset, factor, k * rows, rows)
        return carry

    lax.fori_loop(0, lists[2 * hold, 0], turn, jnp.int32(0))


def scatter_kernel(
    n, rest_ref, resid_ref, x2_ref, hi_ref, margin_ref, owner_ref, rank_ref, loss_ref,
    sum_ref, notes_ref,
    notes, factors, acc, part, crossed, paired, held, send, recv, xsend, xrecv, nsend, nrecv,
):
    ex = margin_ref.shape[1]
    me, side, spot, partner, far = seat(n)
    deep = n // 2
    rows, width = sum_ref.shape
    others = [lax.rem(me + k, n) for k in range(1, n)]
    joined = call_out("rows", others)
    mine = own_lanes()
    steady = ex // GROUP
    tall = jnp.broadcast_to(resid_ref[...], (LANES, ex)).T
    for t in range(steady):
        parts = [
            jnp.sum(
                jnp.where(mine, tall[t * GROUP + h * PER : t * GROUP + (h + 1) * PER, :], 0.0), axis=0, keepdims=True
            )
            for h in range(GROUP // PER)
        ]
        factors[t] = jnp.concatenate(parts, axis=1)

    def gather_pair(j, z):
        acc[...] = rest_ref[pl.ds(pl.multiple_of(z * rows, rows), rows), :]

        def turn(t, carry):
            factor = jnp.broadcast_to(factors[t], (8, WIDE))
            acc[...] += spread_sum(x2_ref[t], offsets(hi_ref[t]), factor, z * rows, rows)
            return carry

        lax.fori_loop(0, steady, turn, jnp.int32(0), unroll=2)
        part[j, 0] = acc[:, 0:width].astype(jnp.bfloat16)
        part[j, 1] = acc[:, width:].astype(jnp.bfloat16)

    def cross(j):
        return send_to("rows", partner, part.at[j, 1 - side], crossed.at[j], xsend.at[j], xrecv.at[j])

    across = []
    along = []

    def pass_on(j):
        across[j].wait_recv()
        pair = part[j, side].astype(jnp.float32) + crossed[j].astype(jnp.float32)
        paired[j] = pair.astype(jnp.bfloat16)
        along.append(
            send_to("rows", 2 * far[j] + side, paired.at[j], held.at[spot], send.at[j], recv.at[spot])
        )

    last = deep - 1
    lead = deep - 2
    gather_pair(0, far[0])
    joined()
    across.append(cross(0))
    for j in range(1, deep):
        gather_pair(j, far[j] if j < last else spot)
        across.append(cross(j))
        if j >= lead:
            pass_on(j - lead)

    which = lax.broadcasted_iota(jnp.int32, (n, ex), 0).astype(jnp.float32)
    by_owner = jnp.where(which == owner_ref[0:1, :], margin_ref[0:1, :], 0.0)
    ordered = lax.dot_general(
        by_owner, rank_ref[...], NT, precision=lax.Precision.HIGHEST, preferred_element_type=jnp.float32
    )
    sub = lax.broadcasted_iota(jnp.int32, (8, LANES), 0)
    for d in range(n):
        notes[d] = jnp.where(sub == 0, ordered[d : d + 1, :], loss_ref[...])
    told = [
        send_to("rows", peer, notes.at[peer], notes_ref.at[me], nsend.at[k], nrecv.at[k])
        for k, peer in enumerate(others)
    ]
    notes_ref[me] = notes[me]
    for j in range(last - lead + 1, last):
        pass_on(j)
    across[last].wait_recv()
    total = part[last, side].astype(jnp.float32) + crossed[last].astype(jnp.float32)
    for z in far[::-1]:
        copy_to("rows", partner, paired.at[0], held.at[z], send.at[0], recv.at[z]).wait_recv()
        total = total + held[z].astype(jnp.float32)
    sum_ref[...] = total
    for copy in across:
        copy.wait_send()
    for copy in along:
        copy.wait_send()
    for copy in told:
        copy.wait()


def finish_kernel(sum_ref, notes_ref, owned_ref, grad_ref, loss_ref):
    n = notes_ref.shape[0]
    ex = owned_ref.shape[1]
    grad_ref[...] = sum_ref[...]
    for h in range(ex // LANES):
        row = jnp.zeros((1, LANES), jnp.float32)
        for d in range(n):
            if d * (ex // n) // LANES == h:
                row = row + notes_ref[d, 0:1, :]
        owned_ref[:, h * LANES : (h + 1) * LANES] = row
    loss = jnp.zeros((1, LANES), jnp.float32)
    for d in range(n):
        loss = loss + notes_ref[d, 1:2, :]
    loss_ref[0, 0] = jnp.sum(loss) * (1.0 / (ex * n))


def on_device(n, nf, tile_values, tile_blocks, tile_counts, labels, owner_rank, weights):
    ex, slots, width = tile_values.shape
    grains = slots // GRAIN
    rows = weights.shape[0]
    deep = n // 2
    turns = ex * grains // GROUP
    steady = ex // GROUP
    hold = -(-(ex * (grains - 1)) // (8 * LANES)) * 8
    f32, i32, bf16 = jnp.float32, jnp.int32, jnp.bfloat16
    shape = jax.ShapeDtypeStruct
    dma = pltpu.SemaphoreType.DMA
    vals = tile_values.reshape(ex * grains, GRAIN, width)

    table, x2, high, lists, rank, owner, first = pl.pallas_call(
        functools.partial(gather_kernel, n),
        out_shape=(
            shape((n, rows, width), bf16),
            shape((turns, 2 * width, WIDE), bf16),
            shape((turns, 1, WIDE), i32),
            shape((3 * hold, LANES), i32),
            shape((LANES, ex), f32),
            shape((8, ex), f32),
            shape((ex, LANES), f32),
        ),
        in_specs=[ANY] * 5,
        out_specs=(VM, VM, VM, SM, VM, VM, VM),
        scratch_shapes=[
            pltpu.VMEM((rows, width), f32),
            pltpu.VMEM((rows, width), bf16),
            pltpu.VMEM((slots, ex), i32),
            pltpu.VMEM((1, ex), i32),
            pltpu.VMEM((1, ex), i32),
            pltpu.VMEM((ex * grains, GRAIN, width), bf16),
            pltpu.VMEM((ex * grains + 8, LANES), i32),
            pltpu.VMEM((3 * hold, LANES), i32),
            pltpu.SMEM((3 * hold, LANES), i32),
            pltpu.VMEM((steady, 8, WIDE), f32),
            dma((deep - 1,)), dma((deep,)), dma((deep,)), dma((deep,)), dma((7,)),
        ],
        compiler_params=pltpu.CompilerParams(collective_id=0, has_side_effects=True, vmem_limit_bytes=GRANT),
        cost_estimate=COST,
    )(*[
        pltpu.with_memory_space_constraint(a, pltpu.HBM)
        for a in (weights, tile_blocks.T, tile_counts.reshape(1, ex), owner_rank.reshape(1, ex), vals)
    ])

    partial = pl.pallas_call(
        margin_kernel,
        out_shape=shape((8, ex), f32),
        in_specs=[SM, VM, VM, VM, VM],
        out_specs=VM,
        scratch_shapes=[pltpu.VMEM((ex * grains + 8, LANES), f32)],
        compiler_params=pltpu.CompilerParams(vmem_limit_bytes=GRANT),
        cost_estimate=COST,
    )(lists, table, x2, high, first)

    margin, resid, loss_part = pl.pallas_call(
        functools.partial(residual_kernel, nf),
        out_shape=(shape((8, ex), f32), shape((1, ex), f32), shape((8, LANES), f32)),
        in_specs=[VM, VM],
        out_specs=(VM, VM, VM),
        scratch_shapes=[pltpu.VMEM((nf, 8, ex), f32), dma((nf - 1,)), dma((nf - 1,))],
        compiler_params=pltpu.CompilerParams(collective_id=1, has_side_effects=True, vmem_limit_bytes=GRANT),
        cost_estimate=COST,
    )(partial, labels.reshape(1, ex))

    rest = pl.pallas_call(
        functools.partial(rest_kernel, grains),
        out_shape=shape((deep * rows, 2 * width), f32),
        in_specs=[SM, SM, VM, VM],
        out_specs=VM,
        compiler_params=pltpu.CompilerParams(vmem_limit_bytes=GRANT),
        cost_estimate=COST,
    )(lists, resid, x2, high)

    total, notes = pl.pallas_call(
        functools.partial(scatter_kernel, n),
        out_shape=(shape((rows, width), f32), shape((n, 8, LANES), f32)),
        in_specs=[VM] * 8,
        out_specs=(VM, VM),
        scratch_shapes=[
            pltpu.VMEM((n, 8, LANES), f32),
            pltpu.VMEM((steady, 1, WIDE), f32),
            pltpu.VMEM((rows, 2 * width), f32),
            pltpu.VMEM((deep, 2, rows, width), bf16),
            pltpu.VMEM((deep, rows, width), bf16),
            pltpu.VMEM((deep - 1, rows, width), bf16),
            pltpu.VMEM((deep, rows, width), bf16),
            dma((deep - 1,)),
            dma((deep,)),
            dma((deep,)),
            dma((deep,)),
            dma((n - 1,)),
            dma((n - 1,)),
        ],
        compiler_params=pltpu.CompilerParams(collective_id=2, has_side_effects=True, vmem_limit_bytes=GRANT),
        cost_estimate=COST,
    )(rest, resid, x2, high, margin, owner, rank, loss_part)

    owned, gradient, loss = pl.pallas_call(
        finish_kernel,
        out_shape=(shape((1, ex), f32), shape((rows, width), f32), shape((1, 1), f32)),
        in_specs=[VM, VM],
        out_specs=(VM, VM, SM),
        compiler_params=pltpu.CompilerParams(vmem_limit_bytes=GRANT),
        cost_estimate=COST,
    )(total, notes)
    return owned.reshape(ex), gradient, loss.reshape(())


def solution(mesh):
    in_specs = (
        P("rows", "feat", None),
        P("rows", "feat"),
        P("rows", "feat"),
        P("rows"),
        P("rows"),
        P(("feat", "rows"), None),
    )
    out_specs = (P("rows"), P(("feat", "rows"), None), P())
    body = functools.partial(on_device, mesh.shape["rows"], mesh.shape["feat"])
    return jax.shard_map(body, mesh=mesh, in_specs=in_specs, out_specs=out_specs, check_vma=False)
```

time: 50.8 us -> 45.2 us (0.89)
  Pallas kernels: 49.7 us -> 44.3 us
    pallas_call x1, Pallas kernels: 5.87 us -> 1.37 us  [on_device(): pl.pallas_call(functools.partial(rest_kernel, grains), out_shape=shape((d...]
    pallas_call x1, Pallas kernels: 17.2 us -> 20.8 us  [on_device(): pl.pallas_call(functools.partial(gather_kernel, n), out_shape=(shape((n,...]
    pallas_call x1, Pallas kernels: 5.07 us -> 1.62 us  [on_device(): pl.pallas_call(margin_kernel, out_shape=shape((8, ex), f32), in_specs=[SM...]
    pallas_call x1, Pallas kernels: 17.1 us -> 16.1 us  [on_device(): pl.pallas_call(functools.partial(scatter_kernel, n), out_shape=(shape((ro...]
where the time goes in v2:
time: 45.2 us; the launch traced here: 45 us
  Pallas kernels  44.3 us (98%)
  between operations  0.69 us (2%)
    pallas_call x1, Pallas kernels, on_device(): pl.pallas_call(functools.partial(gather_kernel, n), out_shape=(shape((n,...  20.8 us
    pallas_call x1, Pallas kernels, on_device(): pl.pallas_call(functools.partial(scatter_kernel, n), out_shape=(shape((ro...  16.1 us
    pallas_call x1, Pallas kernels, on_device(): pl.pallas_call(functools.partial(residual_kernel, nf), out_shape=(shape((...  3.78 us
    pallas_call x1, Pallas kernels, on_device(): pl.pallas_call(margin_kernel, out_shape=shape((8, ex), f32), in_specs=[SM...  1.62 us
    pallas_call x1, Pallas kernels, on_device(): pl.pallas_call(functools.partial(rest_kernel, grains), out_shape=shape((d...  1.37 us

profile of v2, /device:TPU:0, one launch (start us, length us, event | category | flops | bytes accessed | tf_op | source)
XLA Modules:
  0.0 45.0 jit_solution(15361534084082994188)
XLA Ops:
  0.6 0.0 copy-start
  0.6 20.8 %shard_map.85 = (bf16[8,256,128]{2,1,0:T(8,128)(2,1)S(1)}, bf16[32,256,512]{2,1,0:T(8,128)(2,1)S(1)}, s32[32,1,512]{2,1,0:T(1,128)S(1)}, s32[24,128]{1,0:T(8,128...) custom-call(f32[256,128]{1,0:T(8,128)} %w_hbm.1, s32[64,256]{1,0:T(8,128)} %bitcast.9, ...), custom_call_target="tpu_custom_call" | custom-call | bytes 25165824 | tf_op jit(solution)/shard_map/pallas_call | solution.py:477
  21.4 1.6 %shard_map.86.partial_ref = f32[8,256]{1,0:T(8,128)S(1)} custom-call(s32[24,128]{1,0:T(8,128)S(1)} %get-tuple-element.18.lists, bf16[8,256,128]{2,1,0:T(8,128)(2,1)S(1)} %get-tuple-element.19.table_ref, bf16[32,256,512]{2,1,0:T(8,128)(2,1)S(1)} %get-tuple-element.20.x2_ref, s32[32,1,512]{2,1,0:T(1,128)S(1)} %get-tuple-element.21.hi_ref, ...), custom_call_target="tpu_custom_call" | custom-call | bytes 25165824 | tf_op jit(solution)/shard_map/pallas_call | solution.py:510
  23.1 0.0 copy-done
  23.1 3.8 %shard_map.87 = (f32[8,256]{1,0:T(8,128)S(1)}, f32[1,256]{1,0:T(1,128)S(1)}, f32[8,128]{1,0:T(8,128)S(1)}) custom-call(f32[8,256]{1,0:T(8,128)S(1)} %shard_map.86.partial_ref, s32[1,256]{1,0:T(1,128)S(1)} %bitcast.7), custom_call_target="tpu_custom_call" | custom-call | bytes 25165824 | tf_op jit(solution)/shard_map/pallas_call | solution.py:520
  26.9 1.4 %shard_map.88.rest_ref = f32[1024,256]{1,0:T(8,128)S(1)} custom-call(s32[24,128]{1,0:T(8,128)S(1)} %get-tuple-element.18.lists, f32[1,256]{1,0:T(1,128)S(1)} %get-tuple-element.23.resid.resid_ref, bf16[32,256,512]{2,1,0:T(8,128)(2,1)S(1)} %get-tuple-element.20.x2_ref, s32[32,1,512]{2,1,0:T(1,128)S(1)} %get-tuple-element.21.hi_ref), custom_call_target="tpu_custom_call" | custom-call | bytes 25165824 | tf_op jit(solution)/shard_map/pallas_call | solution.py:530
  28.2 16.1 %shard_map.89 = (f32[256,128]{1,0:T(8,128)S(1)}, f32[8,8,128]{2,1,0:T(8,128)S(1)}) custom-call(f32[1024,256]{1,0:T(8,128)S(1)} %shard_map.88.rest_ref, f32[1,256]{1,0:T(1,128)S(1)} %get-tuple-element.23.resid.resid_ref, bf16[32,256,512]{2,1,0:T(8,128)(2,1)S(1)} %get-tuple-element.20.x2_ref, s32[32,1,512]{2,1,0:T(1,128)S(1)} %get-tuple-element.21.hi_ref, ...), custom_call_target="tpu_custom_call" | custom-call | bytes 25165824 | tf_op jit(solution)/shard_map/pallas_call | solution.py:539
  44.3 0.7 %shard_map.90 = (f32[1,256]{1,0:T(1,128)}, f32[256,128]{1,0:T(8,128)}, f32[1,1]{1,0:T(1,128)}) custom-call(f32[256,128]{1,0:T(8,128)S(1)} %get-tuple-element.28.sum_ref, f32[8,8,128]{2,1,0:T(8,128)S(1)} %get-tuple-element.29.notes_ref), custom_call_target="tpu_custom_call" | custom-call | bytes 25165824 | tf_op jit(solution)/shard_map/pallas_call | solution.py:563
Async XLA Ops:
  0.6 22.4 %copy-start = (s32[256]{0:T(256)S(1)}, s32[256]{0:T(256)}, u32[]{:S(2)}) copy-start(s32[256]{0:T(256)} %param.9) | copy-start | bytes 3076

commit v3 on v2

--- a/solution.py
+++ b/solution.py
@@ -21,6 +21,7 @@
 WIDE = GROUP * GRAIN
 PER = LANES // GRAIN
 CUT = 256
+TOGETHER = 2
 
 
 def seat(n):
@@ -29,14 +30,20 @@
     spot = me // 2
     partner = me + 1 - 2 * side
     deep = n // 2
-    tables = [sorted((z for z in range(deep) if z != at), key=lambda z: -abs(z - at)) for at in range(deep)]
-    far = []
-    for j in range(deep - 1):
-        pick = tables[0][j]
-        for at in range(1, deep):
-            pick = pick + (tables[at][j] - tables[at - 1][j]) * ((spot + deep - at) // deep)
-        far.append(pick)
-    return me, side, spot, partner, far
+
+    def listed(key):
+        tables = [sorted((z for z in range(deep) if z != at), key=functools.partial(key, at)) for at in range(deep)]
+        out = []
+        for j in range(deep - 1):
+            pick = tables[0][j]
+            for at in range(1, deep):
+                pick = pick + (tables[at][j] - tables[at - 1][j]) * ((spot + deep - at) // deep)
+            out.append(pick)
+        return out
+
+    far = listed(lambda at, z: -abs(z - at))
+    first = listed(lambda at, z: (abs(z - at)!=1, -abs(z - at)))
+    return me, side, spot, partner, far, first
 
 
 def call_out(axis, peers):
@@ -83,17 +90,45 @@
     return found
 
 
-def spread_sum(x2, offset, factor, first, rows):
+def spread_sum(x2, offset, factor, firsts, rows):
     spread = jnp.concatenate(
-        [jnp.where(offset == first + i * 8, factor, 0.0) for i in range(rows // 8)], axis=0
+        [jnp.where(offset == first + i * 8, factor, 0.0) for first in firsts for i in range(rows // 8)], axis=0
     ).astype(jnp.bfloat16)
     return lax.dot_general(spread, x2, NT, preferred_element_type=jnp.float32)
 
 
+def put(x2_ref, hi_ref, t, values, id_row, rows):
+    tall = x2_ref.shape[1] // 2
+    chunk = id_row // rows
+    odd = lax.rem(chunk, 2)
+    hi_ref[t] = jnp.where(id_row < 0, -1, (chunk // 2) * rows + lax.rem(id_row, rows))
+    odd = jnp.broadcast_to(odd.astype(jnp.float32), (16, WIDE))
+    odd_half = jnp.concatenate([odd.astype(jnp.bfloat16)] * (tall // 16), axis=0)
+    even_half = jnp.concatenate([(1.0 - odd).astype(jnp.bfloat16)] * (tall // 16), axis=0)
+    flipped = values.T
+    x2_ref[t, 0:tall, :] = flipped * even_half
+    x2_ref[t, tall:, :] = flipped * odd_half
+
+
+def listed_tiles(vals, idt, lists, t):
+    hold = lists.shape[0] // 3
+    row = t * GROUP // LANES
+    col = lax.rem(t * GROUP, LANES)
+    group = lane_group()
+    values = jnp.concatenate([vals[lists[row, col + i]] for i in range(GROUP)], axis=0)
+    parts = []
+    for h in range(GROUP // PER):
+        line = idt[pl.ds(lists[hold + row, col + h * PER], 1), :]
+        for i in range(1, PER):
+            line = jnp.where(group == i, idt[pl.ds(lists[hold + row, col + h * PER + i], 1), :], line)
+        parts.append(line)
+    return values, jnp.concatenate(parts, axis=1)
+
+
 def gather_kernel(
     n, w_hbm, ids_hbm, used_hbm, owner_hbm, vals_hbm,
-    table_ref, x2_ref, hi_ref, lists_ref, rank_ref, owner_ref, first_ref,
-    w_buf, half, ids, used, own, vals, idt, lists, glist, found,
+    table_ref, x2_ref, hi_ref, lists_ref, rank_ref, owner_ref, first_ref, vals, idt,
+    w_buf, half, ids, used, own, lists, glist, found,
     send, recv, xsend, xrecv, here,
 ):
     local = [
@@ -105,7 +140,7 @@
     ]
     for copy in local:
         copy.start()
-    me, side, spot, partner, far = seat(n)
+    me, side, spot, partner, far, first = seat(n)
     deep = n // 2
     rows = w_buf.shape[0]
     slots, ex = ids.shape
@@ -117,7 +152,7 @@
     across = [send_to("rows", partner, half, table_ref.at[me], xsend.at[spot], xrecv.at[spot])]
     along = [
         send_to("rows", 2 * z + side, half, table_ref.at[me], send.at[j], recv.at[spot])
-        for j, z in enumerate(far)
+        for j, z in enumerate(first)
     ]
     table_ref[me] = w_buf[...].astype(jnp.bfloat16)
 
@@ -166,22 +201,7 @@
         idt[q * ex : (q + 1) * ex, :] = piece - 1
     idt[grains * ex :, :] = jnp.full((8, LANES), -1, jnp.int32)
 
-    tall = x2_ref.shape[1] // 2
-
-    def put(t, values, id_row):
-        chunk = id_row // rows
-        odd = lax.rem(chunk, 2)
-        high = jnp.where(id_row < 0, -1, (chunk // 2) * rows + lax.rem(id_row, rows))
-        hi_ref[t] = high
-        odd = jnp.broadcast_to(odd.astype(f32), (16, WIDE))
-        odd_half = jnp.concatenate([odd.astype(jnp.bfloat16)] * (tall // 16), axis=0)
-        even_half = jnp.concatenate([(1.0 - odd).astype(jnp.bfloat16)] * (tall // 16), axis=0)
-        flipped = values.T
-        x2_ref[t, 0:tall, :] = flipped * even_half
-        x2_ref[t, tall:, :] = flipped * odd_half
-
     mine = own_lanes()
-    group = lane_group()
     steady = ex // GROUP
 
     def prepare_first(t, carry):
@@ -191,21 +211,13 @@
             jnp.sum(jnp.where(mine, idt[pl.ds(at + h * PER, PER), :], 0), axis=0, keepdims=True)
             for h in range(GROUP // PER)
         ]
-        put(t, values, jnp.concatenate(parts, axis=1))
+        put(x2_ref, hi_ref, t, values, jnp.concatenate(parts, axis=1), rows)
         found[t] = jnp.zeros((8, WIDE), f32)
         return carry
 
     def prepare_rest(t, carry):
-        row = t * GROUP // LANES
-        col = lax.rem(t * GROUP, LANES)
-        values = jnp.concatenate([vals[glist[row, col + i]] for i in range(GROUP)], axis=0)
-        parts = []
-        for h in range(GROUP // PER):
-            line = idt[pl.ds(glist[hold + row, col + h * PER], 1), :]
-            for i in range(1, PER):
-                line = jnp.where(group == i, idt[pl.ds(glist[hold + row, col + h * PER + i], 1), :], line)
-            parts.append(line)
-        put(steady + t, values, jnp.concatenate(parts, axis=1))
+        values, id_row = listed_tiles(vals, idt, glist, t)
+        put(x2_ref, hi_ref, steady + t, values, id_row, rows)
         return carry
 
     def score(z):
@@ -229,17 +241,14 @@
         return copy_to("rows", partner, half, table_ref.at[2 * z + 1 - side], send.at[0], xrecv.at[z])
 
     near = far[::-1]
-    total = x2_ref.shape[0] - steady
-    cuts = [total * j // (deep - 1) for j in range(deep)]
-    cuts = [c // 2 * 2 for c in cuts[:-1]] + [total]
+    lax.fori_loop(0, x2_ref.shape[0] - steady, prepare_rest, jnp.int32(0), unroll=2)
     for j, z in enumerate(near):
         arrival(z).wait_recv()
         block = table_ref.at[2 * z + side]
         across.append(send_to("rows", partner, block, block, xsend.at[z], xrecv.at[z]))
-        lax.fori_loop(cuts[j], cuts[j + 1], prepare_rest, jnp.int32(0), unroll=2 if deep == 4 else 1)
-        done = spot if j == 0 else near[j - 1]
-        crossing(done).wait_recv()
-        score(done)
+        if j == 0:
+            crossing(spot).wait_recv()
+            score(spot)
 
     local[3].wait()
     owner = own[...].astype(f32)
@@ -252,8 +261,9 @@
     rank_ref[...] = jnp.where(places == rank, 1.0, 0.0)
     owner_ref[...] = jnp.broadcast_to(owner, owner_ref.shape)
 
-    crossing(near[-1]).wait_recv()
-    score(near[-1])
+    for z in near:
+        crossing(z).wait_recv()
+        score(z)
     for t in range(steady):
         term = jnp.sum(found[t], axis=0, keepdims=True)
         for h in range(GROUP // PER):
@@ -265,18 +275,20 @@
         copy.wait_send()
 
 
-def margin_kernel(lists, table_ref, x2_ref, hi_ref, first_ref, partial_ref, terms):
+def margin_kernel(
+    lists, table_ref, x2_ref, hi_ref, first_ref, vals, idt, partial_ref, more_x2, more_hi, terms
+):
     n, rows, _ = table_ref.shape
     ex = partial_ref.shape[1]
     grains = terms.shape[0] // ex
     hold = lists.shape[0] // 3
     steady = ex // GROUP
+    ready = x2_ref.shape[0] - steady
     terms[ex:, :] = jnp.zeros((terms.shape[0] - ex, LANES), jnp.float32)
     group = lane_group()
 
-    def one(t):
-        x2 = x2_ref[steady + t]
-        offset = offsets(hi_ref[steady + t])
+    def one(x2, row):
+        offset = offsets(row)
         found = jnp.zeros((8, WIDE), jnp.float32)
         for k in range(n // 2):
             pair = jnp.concatenate([table_ref[2 * k], table_ref[2 * k + 1]], axis=1)
@@ -292,13 +304,21 @@
             terms[pl.ds(lists[hold + row, col + i], 1), :] = mine
 
     def turn(t, carry):
-        a = one(2 * t)
-        b = one(2 * t + 1)
+        a = one(x2_ref[steady + 2 * t], hi_ref[steady + 2 * t])
+        b = one(x2_ref[steady + 2 * t + 1], hi_ref[steady + 2 * t + 1])
         keep(2 * t, a)
         keep(2 * t + 1, b)
         return carry
 
-    lax.fori_loop(0, (lists[2 * hold, 0] + 1) // 2, turn, jnp.int32(0))
+    def late_turn(t, carry):
+        values, id_row = listed_tiles(vals, idt, lists, t)
+        put(more_x2, more_hi, t - ready, values, id_row, rows)
+        keep(t, one(more_x2[t - ready], more_hi[t - ready]))
+        return carry
+
+    turns = lists[2 * hold, 0]
+    lax.fori_loop(0, (jnp.minimum(turns, ready) + 1) // 2, turn, jnp.int32(0))
+    lax.fori_loop(ready, turns, late_turn, jnp.int32(0))
     spread = first_ref[...]
     for q in range(1, grains):
         spread = spread + terms[q * ex : (q + 1) * ex, :]
@@ -330,16 +350,15 @@
     loss_ref[...] = total
 
 
-def rest_kernel(grains, lists, resid, x2_ref, hi_ref, total):
+def rest_kernel(grains, lists, resid, x2_ref, hi_ref, more_x2, more_hi, total):
     total[...] = jnp.zeros_like(total)
     hold = lists.shape[0] // 3
     rows = CUT
     steady = resid.shape[1] // GROUP
+    ready = x2_ref.shape[0] - steady
     group = lane_group()
 
-    def turn(t, carry):
-        x2 = x2_ref[steady + t]
-        offset = offsets(hi_ref[steady + t])
+    def factor_of(t):
         row_at = t * GROUP // LANES
         col = lax.rem(t * GROUP, LANES)
         parts = []
@@ -348,12 +367,28 @@
             for i in range(PER):
                 row = jnp.where(group == i, resid[0, lists[row_at, col + h * PER + i] // grains], row)
             parts.append(row)
-        factor = jnp.broadcast_to(jnp.concatenate(parts, axis=1), (8, WIDE))
+        return jnp.broadcast_to(jnp.concatenate(parts, axis=1), (8, WIDE))
+
+    def turn(t, carry):
+        at = steady + 2 * t
+        x2a, x2b = x2_ref[at], x2_ref[at + 1]
+        offset_a, offset_b = offsets(hi_ref[at]), offsets(hi_ref[at + 1])
+        factor_a, factor_b = factor_of(2 * t), factor_of(2 * t + 1)
         for k in range(total.shape[0] // rows):
-            total[k * rows : (k + 1) * rows, :] += spread_sum(x2, offset, factor, k * rows, rows)
+            total[k * rows : (k + 1) * rows, :] += spread_sum(
+                x2a, offset_a, factor_a, [k * rows], rows
+            ) + spread_sum(x2b, offset_b, factor_b, [k * rows], rows)
         return carry
 
-    lax.fori_loop(0, lists[2 * hold, 0], turn, jnp.int32(0))
+    def late_turn(t, carry):
+        x2, offset, factor = more_x2[t - ready], offsets(more_hi[t - ready]), factor_of(t)
+        for k in range(total.shape[0] // rows):
+            total[k * rows : (k + 1) * rows, :] += spread_sum(x2, offset, factor, [k * rows], rows)
+        return carry
+
+    turns = lists[2 * hold, 0]
+    lax.fori_loop(0, (jnp.minimum(turns, ready) + 1) // 2, turn, jnp.int32(0))
+    lax.fori_loop(ready, turns, late_turn, jnp.int32(0))
 
 
 def scatter_kernel(
@@ -362,7 +397,7 @@
     notes, factors, acc, part, crossed, paired, held, send, recv, xsend, xrecv, nsend, nrecv,
 ):
     ex = margin_ref.shape[1]
-    me, side, spot, partner, far = seat(n)
+    me, side, spot, partner, far, first = seat(n)
     deep = n // 2
     rows, width = sum_ref.shape
     others = [lax.rem(me + k, n) for k in range(1, n)]
@@ -379,17 +414,20 @@
         ]
         factors[t] = jnp.concatenate(parts, axis=1)
 
-    def gather_pair(j, z):
-        acc[...] = rest_ref[pl.ds(pl.multiple_of(z * rows, rows), rows), :]
+    def gather_pairs(js, zs):
+        for i, z in enumerate(zs):
+            acc[i * rows : (i + 1) * rows, :] = rest_ref[pl.ds(pl.multiple_of(z * rows, rows), rows), :]
+        high = len(js) * rows
 
         def turn(t, carry):
             factor = jnp.broadcast_to(factors[t], (8, WIDE))
-            acc[...] += spread_sum(x2_ref[t], offsets(hi_ref[t]), factor, z * rows, rows)
+            acc[0:high, :] += spread_sum(x2_ref[t], offsets(hi_ref[t]), factor, [z * rows for z in zs], rows)
             return carry
 
         lax.fori_loop(0, steady, turn, jnp.int32(0), unroll=2)
-        part[j, 0] = acc[:, 0:width].astype(jnp.bfloat16)
-        part[j, 1] = acc[:, width:].astype(jnp.bfloat16)
+        for i, j in enumerate(js):
+            part[j, 0] = acc[i * rows : (i + 1) * rows, 0:width].astype(jnp.bfloat16)
+            part[j, 1] = acc[i * rows : (i + 1) * rows, width:].astype(jnp.bfloat16)
 
     def cross(j):
         return send_to("rows", partner, part.at[j, 1 - side], crossed.at[j], xsend.at[j], xrecv.at[j])
@@ -406,15 +444,13 @@
         )
 
     last = deep - 1
-    lead = deep - 2
-    gather_pair(0, far[0])
-    joined()
-    across.append(cross(0))
-    for j in range(1, deep):
-        gather_pair(j, far[j] if j < last else spot)
-        across.append(cross(j))
-        if j >= lead:
-            pass_on(j - lead)
+    planes = far + [spot]
+    for j in range(0, deep, TOGETHER):
+        js = list(range(j, min(j + TOGETHER, deep)))
+        gather_pairs(js, [planes[i] for i in js])
+        if j == 0:
+            joined()
+        across += [cross(i) for i in js]
 
     which = lax.broadcasted_iota(jnp.int32, (n, ex), 0).astype(jnp.float32)
     by_owner = jnp.where(which == owner_ref[0:1, :], margin_ref[0:1, :], 0.0)
@@ -429,7 +465,7 @@
         for k, peer in enumerate(others)
     ]
     notes_ref[me] = notes[me]
-    for j in range(last - lead + 1, last):
+    for j in range(last):
         pass_on(j)
     across[last].wait_recv()
     total = part[last, side].astype(jnp.float32) + crossed[last].astype(jnp.float32)
@@ -466,35 +502,35 @@
     grains = slots // GRAIN
     rows = weights.shape[0]
     deep = n // 2
-    turns = ex * grains // GROUP
     steady = ex // GROUP
+    late = max((grains - 2) * steady, 1)
     hold = -(-(ex * (grains - 1)) // (8 * LANES)) * 8
     f32, i32, bf16 = jnp.float32, jnp.int32, jnp.bfloat16
     shape = jax.ShapeDtypeStruct
     dma = pltpu.SemaphoreType.DMA
     vals = tile_values.reshape(ex * grains, GRAIN, width)
 
-    table, x2, high, lists, rank, owner, first = pl.pallas_call(
+    table, x2, high, lists, rank, owner, first, packed, named = pl.pallas_call(
         functools.partial(gather_kernel, n),
         out_shape=(
             shape((n, rows, width), bf16),
-            shape((turns, 2 * width, WIDE), bf16),
-            shape((turns, 1, WIDE), i32),
+            shape((2 * steady, 2 * width, WIDE), bf16),
+            shape((2 * steady, 1, WIDE), i32),
             shape((3 * hold, LANES), i32),
             shape((LANES, ex), f32),
             shape((8, ex), f32),
             shape((ex, LANES), f32),
+            shape((ex * grains, GRAIN, width), bf16),
+            shape((ex * grains + 8, LANES), i32),
         ),
         in_specs=[ANY] * 5,
-        out_specs=(VM, VM, VM, SM, VM, VM, VM),
+        out_specs=(VM, VM, VM, SM, VM, VM, VM, VM, VM),
         scratch_shapes=[
             pltpu.VMEM((rows, width), f32),
             pltpu.VMEM((rows, width), bf16),
             pltpu.VMEM((slots, ex), i32),
             pltpu.VMEM((1, ex), i32),
             pltpu.VMEM((1, ex), i32),
-            pltpu.VMEM((ex * grains, GRAIN, width), bf16),
-            pltpu.VMEM((ex * grains + 8, LANES), i32),
             pltpu.VMEM((3 * hold, LANES), i32),
             pltpu.SMEM((3 * hold, LANES), i32),
             pltpu.VMEM((steady, 8, WIDE), f32),
@@ -507,15 +543,15 @@
         for a in (weights, tile_blocks.T, tile_counts.reshape(1, ex), owner_rank.reshape(1, ex), vals)
     ])
 
-    partial = pl.pallas_call(
+    partial, more_x2, more_high = pl.pallas_call(
         margin_kernel,
-        out_shape=shape((8, ex), f32),
-        in_specs=[SM, VM, VM, VM, VM],
-        out_specs=VM,
+        out_shape=(shape((8, ex), f32), shape((late, 2 * width, WIDE), bf16), shape((late, 1, WIDE), i32)),
+        in_specs=[SM] + [VM] * 6,
+        out_specs=(VM, VM, VM),
         scratch_shapes=[pltpu.VMEM((ex * grains + 8, LANES), f32)],
         compiler_params=pltpu.CompilerParams(vmem_limit_bytes=GRANT),
         cost_estimate=COST,
-    )(lists, table, x2, high, first)
+    )(lists, table, x2, high, first, packed, named)
 
     margin, resid, loss_part = pl.pallas_call(
         functools.partial(residual_kernel, nf),
@@ -530,11 +566,11 @@
     rest = pl.pallas_call(
         functools.partial(rest_kernel, grains),
         out_shape=shape((deep * rows, 2 * width), f32),
-        in_specs=[SM, SM, VM, VM],
+        in_specs=[SM, SM, VM, VM, VM, VM],
         out_specs=VM,
         compiler_params=pltpu.CompilerParams(vmem_limit_bytes=GRANT),
         cost_estimate=COST,
-    )(lists, resid, x2, high)
+    )(lists, resid, x2, high, more_x2, more_high)
 
     total, notes = pl.pallas_call(
         functools.partial(scatter_kernel, n),
@@ -544,7 +580,7 @@
         scratch_shapes=[
             pltpu.VMEM((n, 8, LANES), f32),
             pltpu.VMEM((steady, 1, WIDE), f32),
-            pltpu.VMEM((rows, 2 * width), f32),
+            pltpu.VMEM((TOGETHER * rows, 2 * width), f32),
             pltpu.VMEM((deep, 2, rows, width), bf16),
             pltpu.VMEM((deep, rows, width), bf16),
             pltpu.VMEM((deep - 1, rows, width), bf16),

time: 45.2 us -> 42.4 us (0.938)
  Pallas kernels: 44.3 us -> 41.6 us
    pallas_call x1, Pallas kernels: 20.8 us -> 19 us  [on_device(): pl.pallas_call(functools.partial(gather_kernel, n), out_shape=(shape((n,...]
    pallas_call x1, Pallas kernels: 16.1 us -> 14.8 us  [on_device(): pl.pallas_call(functools.partial(scatter_kernel, n), out_shape=(shape((ro...]
where the time goes in v3:
time: 42.4 us; the launch traced here: 42.3 us
  Pallas kernels  41.6 us (98%)
  between operations  0.69 us (2%)
    pallas_call x1, Pallas kernels, on_device(): pl.pallas_call(functools.partial(gather_kernel, n), out_shape=(shape((n,...  19 us
    pallas_call x1, Pallas kernels, on_device(): pl.pallas_call(functools.partial(scatter_kernel, n), out_shape=(shape((ro...  14.8 us
    pallas_call x1, Pallas kernels, on_device(): pl.pallas_call(functools.partial(residual_kernel, nf), out_shape=(shape((...  3.78 us
    pallas_call x1, Pallas kernels, on_device(): pl.pallas_call(functools.partial(rest_kernel, grains), out_shape=shape((d...  1.75 us
    pallas_call x1, Pallas kernels, on_device(): pl.pallas_call(margin_kernel, out_shape=(shape((8, ex), f32), shape((late...  1.63 us

profile of v3, /device:TPU:0, one launch (start us, length us, event | category | flops | bytes accessed | tf_op | source)
XLA Modules:
  0.0 42.3 jit_solution(9845768818528685520)
XLA Ops:
  0.6 19.0 %shard_map.85 = (bf16[8,256,128]{2,1,0:T(8,128)(2,1)S(1)}, bf16[16,256,512]{2,1,0:T(8,128)(2,1)S(1)}, s32[16,1,512]{2,1,0:T(1,128)S(1)}, s32[24,128]{1,0:T(8,128...) custom-call(f32[256,128]{1,0:T(8,128)} %w_hbm.1, ...), custom_call_target="tpu_custom_call" | custom-call | bytes 25165824 | tf_op jit(solution)/shard_map/pallas_call | solution.py:513
  19.6 0.0 copy-start
  19.6 1.6 %shard_map.86 = (f32[8,256]{1,0:T(8,128)S(1)}, bf16[16,256,512]{2,1,0:T(8,128)(2,1)S(1)}, s32[16,1,512]{2,1,0:T(1,128)S(1)}) custom-call(s32[24,128]{1,0:T(8,128)S(1)} %get-tuple-element.23.lists, bf16[8,256,128]{2,1,0:T(8,128)(2,1)S(1)} %get-tuple-element.24.table_ref, bf16[16,256,512]{2,1,0:T(8,128)(2,1)S(1)} %get-tuple-element.25.x2_ref, ...), custom_call_target="tpu_custom_call" | custom-call | bytes 25165824 | tf_op jit(solution)/shard_map/pallas_call | solution.py:546
  21.3 0.0 copy-done
  21.3 3.8 %shard_map.87 = (f32[8,256]{1,0:T(8,128)S(1)}, f32[1,256]{1,0:T(1,128)S(1)}, f32[8,128]{1,0:T(8,128)S(1)}) custom-call(f32[8,256]{1,0:T(8,128)S(1)} %get-tuple-element.30.partial_ref, s32[1,256]{1,0:T(1,128)S(1)} %bitcast.7), custom_call_target="tpu_custom_call" | custom-call | bytes 25165824 | tf_op jit(solution)/shard_map/pallas_call | solution.py:556
  25.1 1.7 %shard_map.88.rest_ref = f32[1024,256]{1,0:T(8,128)S(1)} custom-call(s32[24,128]{1,0:T(8,128)S(1)} %get-tuple-element.23.lists, f32[1,256]{1,0:T(1,128)S(1)} %get-tuple-element.31.resid.resid_ref, bf16[16,256,512]{2,1,0:T(8,128)(2,1)S(1)} %get-tuple-element.25.x2_ref, s32[16,1,512]{2,1,0:T(1,128)S(1)} %get-tuple-element.26.hi_ref, ...), custom_call_target="tpu_custom_call" | custom-call | bytes 25165824 | tf_op jit(solution)/shard_map/pallas_call | solution.py:566
  26.8 14.8 %shard_map.89 = (f32[256,128]{1,0:T(8,128)S(1)}, f32[8,8,128]{2,1,0:T(8,128)S(1)}) custom-call(f32[1024,256]{1,0:T(8,128)S(1)} %shard_map.88.rest_ref, f32[1,256]{1,0:T(1,128)S(1)} %get-tuple-element.31.resid.resid_ref, bf16[16,256,512]{2,1,0:T(8,128)(2,1)S(1)} %get-tuple-element.25.x2_ref, s32[16,1,512]{2,1,0:T(1,128)S(1)} %get-tuple-element.26.hi_ref, ...), custom_call_target="tpu_custom_call" | custom-call | bytes 25165824 | tf_op jit(solution)/shard_map/pallas_call | solution.py:575
  41.6 0.7 %shard_map.90 = (f32[1,256]{1,0:T(1,128)}, f32[256,128]{1,0:T(8,128)}, f32[1,1]{1,0:T(1,128)}) custom-call(f32[256,128]{1,0:T(8,128)S(1)} %get-tuple-element.38.sum_ref, f32[8,8,128]{2,1,0:T(8,128)S(1)} %get-tuple-element.39.notes_ref), custom_call_target="tpu_custom_call" | custom-call | bytes 25165824 | tf_op jit(solution)/shard_map/pallas_call | solution.py:599
Async XLA Ops:
  19.6 1.6 %copy-start = (s32[256]{0:T(256)S(1)}, s32[256]{0:T(256)}, u32[]{:S(2)}) copy-start(s32[256]{0:T(256)} %param.9) | copy-start | bytes 3076

commit v4 on v3

--- a/solution.py
+++ b/solution.py
@@ -20,7 +20,8 @@
 ANY = pl.BlockSpec(memory_space=pltpu.HBM)
 WIDE = GROUP * GRAIN
 PER = LANES // GRAIN
-CUT = 256
+CUT = 512
+BATCH = 7
 TOGETHER = 2
 
 
@@ -127,7 +128,7 @@
 
 def gather_kernel(
     n, w_hbm, ids_hbm, used_hbm, owner_hbm, vals_hbm,
-    table_ref, x2_ref, hi_ref, lists_ref, rank_ref, owner_ref, first_ref, vals, idt,
+    table_ref, x2_ref, hi_ref, lists_ref, rank_ref, owner_ref, first_ref, rest_ref, vals, idt,
     w_buf, half, ids, used, own, lists, glist, found,
     send, recv, xsend, xrecv, here,
 ):
@@ -218,6 +219,7 @@
     def prepare_rest(t, carry):
         values, id_row = listed_tiles(vals, idt, glist, t)
         put(x2_ref, hi_ref, steady + t, values, id_row, rows)
+        found[steady + t] = jnp.zeros((8, WIDE), f32)
         return carry
 
     def score(z):
@@ -227,7 +229,7 @@
             found[t] = select_scores(pair, x2_ref[t], offsets(hi_ref[t]), z * rows, found[t])
             return carry
 
-        lax.fori_loop(0, steady, turn, jnp.int32(0), unroll=2)
+        lax.fori_loop(0, x2_ref.shape[0], turn, jnp.int32(0), unroll=True)
 
     local[4].wait()
     lax.fori_loop(0, steady, prepare_first, jnp.int32(0), unroll=2)
@@ -269,6 +271,8 @@
         for h in range(GROUP // PER):
             at = t * GROUP + h * PER
             first_ref[at : at + PER, :] = jnp.where(mine, term[:, h * LANES : (h + 1) * LANES], 0.0)
+    for t in range(x2_ref.shape[0] - steady):
+        rest_ref[t] = jnp.sum(found[steady + t], axis=0, keepdims=True)
     for copy in along:
         copy.wait_send()
     for copy in across:
@@ -276,14 +280,13 @@
 
 
 def margin_kernel(
-    lists, table_ref, x2_ref, hi_ref, first_ref, vals, idt, partial_ref, more_x2, more_hi, terms
+    lists, table_ref, first_ref, rest_ref, vals, idt, partial_ref, more_x2, more_hi, terms
 ):
     n, rows, _ = table_ref.shape
     ex = partial_ref.shape[1]
     grains = terms.shape[0] // ex
     hold = lists.shape[0] // 3
-    steady = ex // GROUP
-    ready = x2_ref.shape[0] - steady
+    ready = rest_ref.shape[0]
     terms[ex:, :] = jnp.zeros((terms.shape[0] - ex, LANES), jnp.float32)
     group = lane_group()
 
@@ -304,10 +307,7 @@
             terms[pl.ds(lists[hold + row, col + i], 1), :] = mine
 
     def turn(t, carry):
-        a = one(x2_ref[steady + 2 * t], hi_ref[steady + 2 * t])
-        b = one(x2_ref[steady + 2 * t + 1], hi_ref[steady + 2 * t + 1])
-        keep(2 * t, a)
-        keep(2 * t + 1, b)
+        keep(t, rest_ref[t])
         return carry
 
     def late_turn(t, carry):
@@ -317,7 +317,7 @@
         return carry
 
     turns = lists[2 * hold, 0]
-    lax.fori_loop(0, (jnp.minimum(turns, ready) + 1) // 2, turn, jnp.int32(0))
+    lax.fori_loop(0, jnp.minimum(turns, ready), turn, jnp.int32(0))
     lax.fori_loop(ready, turns, late_turn, jnp.int32(0))
     spread = first_ref[...]
     for q in range(1, grains):
@@ -350,51 +350,39 @@
     loss_ref[...] = total
 
 
-def rest_kernel(grains, lists, resid, x2_ref, hi_ref, more_x2, more_hi, total):
-    total[...] = jnp.zeros_like(total)
-    hold = lists.shape[0] // 3
-    rows = CUT
-    steady = resid.shape[1] // GROUP
-    ready = x2_ref.shape[0] - steady
+def factor_row(grains, lists, resid, t):
     group = lane_group()
-
-    def factor_of(t):
-        row_at = t * GROUP // LANES
-        col = lax.rem(t * GROUP, LANES)
-        parts = []
-        for h in range(GROUP // PER):
-            row = jnp.zeros((1, LANES), jnp.float32)
-            for i in range(PER):
-                row = jnp.where(group == i, resid[0, lists[row_at, col + h * PER + i] // grains], row)
-            parts.append(row)
-        return jnp.broadcast_to(jnp.concatenate(parts, axis=1), (8, WIDE))
+    row_at = t * GROUP // LANES
+    col = lax.rem(t * GROUP, LANES)
+    parts = []
+    for h in range(GROUP // PER):
+        row = jnp.zeros((1, LANES), jnp.float32)
+        for i in range(PER):
+            row = jnp.where(group == i, resid[0, lists[row_at, col + h * PER + i] // grains], row)
+        parts.append(row)
+    return jnp.concatenate(parts, axis=1)
+
+
+def late_kernel(grains, ready, lists, resid, more_x2, more_hi, total):
+    turns = lists[lists.shape[0] // 3 * 2, 0]
 
     def turn(t, carry):
-        at = steady + 2 * t
-        x2a, x2b = x2_ref[at], x2_ref[at + 1]
-        offset_a, offset_b = offsets(hi_ref[at]), offsets(hi_ref[at + 1])
-        factor_a, factor_b = factor_of(2 * t), factor_of(2 * t + 1)
-        for k in range(total.shape[0] // rows):
-            total[k * rows : (k + 1) * rows, :] += spread_sum(
-                x2a, offset_a, factor_a, [k * rows], rows
-            ) + spread_sum(x2b, offset_b, factor_b, [k * rows], rows)
+        factor = jnp.broadcast_to(factor_row(grains, lists, resid, t), (8, WIDE))
+        x2, offset = more_x2[t - ready], offsets(more_hi[t - ready])
+        for k in range(0, total.shape[0], CUT):
+            total[k : k + CUT, :] += spread_sum(x2, offset, factor, [k], CUT)
         return carry
 
-    def late_turn(t, carry):
-        x2, offset, factor = more_x2[t - ready], offsets(more_hi[t - ready]), factor_of(t)
-        for k in range(total.shape[0] // rows):
-            total[k * rows : (k + 1) * rows, :] += spread_sum(x2, offset, factor, [k * rows], rows)
-        return carry
-
-    turns = lists[2 * hold, 0]
-    lax.fori_loop(0, (jnp.minimum(turns, ready) + 1) // 2, turn, jnp.int32(0))
-    lax.fori_loop(ready, turns, late_turn, jnp.int32(0))
+    @pl.when(turns > ready)
+    def _():
+        total[...] = jnp.zeros_like(total)
+        lax.fori_loop(ready, turns, turn, jnp.int32(0))
 
 
 def scatter_kernel(
-    n, rest_ref, resid_ref, x2_ref, hi_ref, margin_ref, owner_ref, rank_ref, loss_ref,
+    n, grains, lists_ref, rest_ref, resid_ref, x2_ref, hi_ref, margin_ref, owner_ref, rank_ref, loss_ref,
     sum_ref, notes_ref,
-    notes, factors, acc, part, crossed, paired, held, send, recv, xsend, xrecv, nsend, nrecv,
+    lists, resid, here, notes, factors, acc, part, crossed, paired, held, send, recv, xsend, xrecv, nsend, nrecv,
 ):
     ex = margin_ref.shape[1]
     me, side, spot, partner, far, first = seat(n)
@@ -402,8 +390,16 @@
     rows, width = sum_ref.shape
     others = [lax.rem(me + k, n) for k in range(1, n)]
     joined = call_out("rows", others)
+    local = [
+        pltpu.make_async_copy(lists_ref, lists, here.at[0]),
+        pltpu.make_async_copy(resid_ref, resid, here.at[1]),
+    ]
+    for copy in local:
+        copy.start()
     mine = own_lanes()
     steady = ex // GROUP
+    ready = x2_ref.shape[0] - steady
+    hold = lists.shape[0] // 3
     tall = jnp.broadcast_to(resid_ref[...], (LANES, ex)).T
     for t in range(steady):
         parts = [
@@ -413,18 +409,35 @@
             for h in range(GROUP // PER)
         ]
         factors[t] = jnp.concatenate(parts, axis=1)
+    for copy in local:
+        copy.wait()
+
+    def listed_factor(t, carry):
+        factors[steady + t] = factor_row(grains, lists, resid, t)
+        return carry
+
+    lax.fori_loop(0, ready, listed_factor, jnp.int32(0), unroll=2)
+    late = jnp.broadcast_to(lists_ref[2 * hold : 2 * hold + 1, 0:1] > ready, (rows, 2 * width))
+
+    batch = max(b for b in range(1, BATCH + 1) if (steady + ready) % b == 0)
 
     def gather_pairs(js, zs):
         for i, z in enumerate(zs):
-            acc[i * rows : (i + 1) * rows, :] = rest_ref[pl.ds(pl.multiple_of(z * rows, rows), rows), :]
+            more = rest_ref[pl.ds(pl.multiple_of(z * rows, rows), rows), :]
+            acc[i * rows : (i + 1) * rows, :] = jnp.where(late, more, 0.0)
         high = len(js) * rows
 
-        def turn(t, carry):
-            factor = jnp.broadcast_to(factors[t], (8, WIDE))
-            acc[0:high, :] += spread_sum(x2_ref[t], offsets(hi_ref[t]), factor, [z * rows for z in zs], rows)
+        def turn(step, carry):
+            part_sum = None
+            for i in range(batch):
+                t = step * batch + i
+                factor = jnp.broadcast_to(factors[t], (8, WIDE))
+                more = spread_sum(x2_ref[t], offsets(hi_ref[t]), factor, [z * rows for z in zs], rows)
+                part_sum = more if part_sum is None else part_sum + more
+            acc[0:high, :] += part_sum
             return carry
 
-        lax.fori_loop(0, steady, turn, jnp.int32(0), unroll=2)
+        lax.fori_loop(0, (steady + ready) // batch, turn, jnp.int32(0))
         for i, j in enumerate(js):
             part[j, 0] = acc[i * rows : (i + 1) * rows, 0:width].astype(jnp.bfloat16)
             part[j, 1] = acc[i * rows : (i + 1) * rows, width:].astype(jnp.bfloat16)
@@ -503,28 +516,30 @@
     rows = weights.shape[0]
     deep = n // 2
     steady = ex // GROUP
-    late = max((grains - 2) * steady, 1)
+    ready = min(6, (grains - 1) * steady)
+    late = max((grains - 1) * steady - ready, 1)
     hold = -(-(ex * (grains - 1)) // (8 * LANES)) * 8
     f32, i32, bf16 = jnp.float32, jnp.int32, jnp.bfloat16
     shape = jax.ShapeDtypeStruct
     dma = pltpu.SemaphoreType.DMA
     vals = tile_values.reshape(ex * grains, GRAIN, width)
 
-    table, x2, high, lists, rank, owner, first, packed, named = pl.pallas_call(
+    table, x2, high, lists, rank, owner, first, found, packed, named = pl.pallas_call(
         functools.partial(gather_kernel, n),
         out_shape=(
             shape((n, rows, width), bf16),
-            shape((2 * steady, 2 * width, WIDE), bf16),
-            shape((2 * steady, 1, WIDE), i32),
+            shape((steady + ready, 2 * width, WIDE), bf16),
+            shape((steady + ready, 1, WIDE), i32),
             shape((3 * hold, LANES), i32),
             shape((LANES, ex), f32),
             shape((8, ex), f32),
             shape((ex, LANES), f32),
+            shape((ready, 1, WIDE), f32),
             shape((ex * grains, GRAIN, width), bf16),
             shape((ex * grains + 8, LANES), i32),
         ),
         in_specs=[ANY] * 5,
-        out_specs=(VM, VM, VM, SM, VM, VM, VM, VM, VM),
+        out_specs=(VM, VM, VM, SM, VM, VM, VM, VM, VM, VM),
         scratch_shapes=[
             pltpu.VMEM((rows, width), f32),
             pltpu.VMEM((rows, width), bf16),
@@ -533,7 +548,7 @@
             pltpu.VMEM((1, ex), i32),
             pltpu.VMEM((3 * hold, LANES), i32),
             pltpu.SMEM((3 * hold, LANES), i32),
-            pltpu.VMEM((steady, 8, WIDE), f32),
+            pltpu.VMEM((steady + ready, 8, WIDE), f32),
             dma((deep - 1,)), dma((deep,)), dma((deep,)), dma((deep,)), dma((7,)),
         ],
         compiler_params=pltpu.CompilerParams(collective_id=0, has_side_effects=True, vmem_limit_bytes=GRANT),
@@ -546,12 +561,12 @@
     partial, more_x2, more_high = pl.pallas_call(
         margin_kernel,
         out_shape=(shape((8, ex), f32), shape((late, 2 * width, WIDE), bf16), shape((late, 1, WIDE), i32)),
-        in_specs=[SM] + [VM] * 6,
+        in_specs=[SM] + [VM] * 5,
         out_specs=(VM, VM, VM),
         scratch_shapes=[pltpu.VMEM((ex * grains + 8, LANES), f32)],
         compiler_params=pltpu.CompilerParams(vmem_limit_bytes=GRANT),
         cost_estimate=COST,
-    )(lists, table, x2, high, first, packed, named)
+    )(lists, table, first, found, packed, named)
 
     margin, resid, loss_part = pl.pallas_call(
         functools.partial(residual_kernel, nf),
@@ -564,22 +579,25 @@
     )(partial, labels.reshape(1, ex))
 
     rest = pl.pallas_call(
-        functools.partial(rest_kernel, grains),
+        functools.partial(late_kernel, grains, ready),
         out_shape=shape((deep * rows, 2 * width), f32),
-        in_specs=[SM, SM, VM, VM, VM, VM],
+        in_specs=[SM, SM, VM, VM],
         out_specs=VM,
         compiler_params=pltpu.CompilerParams(vmem_limit_bytes=GRANT),
         cost_estimate=COST,
-    )(lists, resid, x2, high, more_x2, more_high)
+    )(lists, resid, more_x2, more_high)
 
     total, notes = pl.pallas_call(
-        functools.partial(scatter_kernel, n),
+        functools.partial(scatter_kernel, n, grains),
         out_shape=(shape((rows, width), f32), shape((n, 8, LANES), f32)),
-        in_specs=[VM] * 8,
+        in_specs=[VM] * 9,
         out_specs=(VM, VM),
         scratch_shapes=[
+            pltpu.SMEM((3 * hold, LANES), i32),
+            pltpu.SMEM((1, ex), f32),
+            dma((2,)),
             pltpu.VMEM((n, 8, LANES), f32),
-            pltpu.VMEM((steady, 1, WIDE), f32),
+            pltpu.VMEM((steady + ready, 1, WIDE), f32),
             pltpu.VMEM((TOGETHER * rows, 2 * width), f32),
             pltpu.VMEM((deep, 2, rows, width), bf16),
             pltpu.VMEM((deep, rows, width), bf16),
@@ -594,7 +612,7 @@
         ],
         compiler_params=pltpu.CompilerParams(collective_id=2, has_side_effects=True, vmem_limit_bytes=GRANT),
         cost_estimate=COST,
-    )(rest, resid, x2, high, margin, owner, rank, loss_part)
+    )(lists, rest, resid, x2, high, margin, owner, rank, loss_part)
 
     owned, gradient, loss = pl.pallas_call(
         finish_kernel,

time: 42.4 us -> 39.6 us (0.934)
  Pallas kernels: 41.6 us -> 38.8 us
    pallas_call x2, Pallas kernels: 16.6 us -> 14.6 us  [the longest x1 13.9 us: on_device(): pl.pallas_call(functools.partial(scatter_kernel, n, grains), out_shape=(s...]
    pallas_call x1, Pallas kernels: 1.63 us -> 0.96 us  [on_device(): pl.pallas_call(margin_kernel, out_shape=(shape((8, ex), f32), shape((late...]
where the time goes in v4:
time: 39.6 us; the launch traced here: 39.5 us
  Pallas kernels  38.8 us (98%)
  between operations  0.69 us (2%)
    pallas_call x1, Pallas kernels, on_device(): pl.pallas_call(functools.partial(gather_kernel, n), out_shape=(shape((n,...  18.7 us
    pallas_call x1, Pallas kernels, on_device(): pl.pallas_call(functools.partial(scatter_kernel, n, grains), out_shape=(s...  13.9 us
    pallas_call x1, Pallas kernels, on_device(): pl.pallas_call(functools.partial(residual_kernel, nf), out_shape=(shape((...  3.78 us
    pallas_call x1, Pallas kernels, on_device(): pl.pallas_call(margin_kernel, out_shape=(shape((8, ex), f32), shape((late...  0.96 us

profile of v4, /device:TPU:0, one launch (start us, length us, event | category | flops | bytes accessed | tf_op | source)
XLA Modules:
  0.0 39.5 jit_solution(12556465899194767118)
XLA Ops:
  0.6 0.0 copy-start
  0.6 18.7 %shard_map.85 = (bf16[8,256,128]{2,1,0:T(8,128)(2,1)S(1)}, bf16[14,256,512]{2,1,0:T(8,128)(2,1)S(1)}, s32[14,1,512]{2,1,0:T(1,128)S(1)}, s32[24,128]{1,0:T(8,128...) custom-call(f32[256,128]{1,0:T(8,128)} %w_hbm.1, ...), custom_call_target="tpu_custom_call" | custom-call | bytes 25165824 | tf_op jit(solution)/shard_map/pallas_call | solution.py:527
  19.4 1.0 %shard_map.86 = (f32[8,256]{1,0:T(8,128)S(1)}, bf16[18,256,512]{2,1,0:T(8,128)(2,1)S(1)}, s32[18,1,512]{2,1,0:T(1,128)S(1)}) custom-call(s32[24,128]{1,0:T(8,128)S(1)} %get-tuple-element.24.lists.lists_ref, bf16[8,256,128]{2,1,0:T(8,128)(2,1)S(1)} %get-tuple-element.25.table_ref, f32[256,128]{1,0:T(8,128)S(1)} %get-tuple-element.26.first_ref, ...), custom_call_target="tpu_custom_call" | custom-call | bytes 25165824 | tf_op jit(solution)/shard_map/pallas_call | solution.py:561
  20.4 0.0 copy-done
  20.4 3.8 %shard_map.87 = (f32[8,256]{1,0:T(8,128)S(1)}, f32[1,256]{1,0:T(1,128)S(1)}, f32[8,128]{1,0:T(8,128)S(1)}) custom-call(f32[8,256]{1,0:T(8,128)S(1)} %get-tuple-element.30.partial_ref, s32[1,256]{1,0:T(1,128)S(1)} %bitcast.7), custom_call_target="tpu_custom_call" | custom-call | bytes 25165824 | tf_op jit(solution)/shard_map/pallas_call | solution.py:571
  24.2 0.8 %shard_map.88.rest_ref = f32[1024,256]{1,0:T(8,128)S(1)} custom-call(s32[24,128]{1,0:T(8,128)S(1)} %get-tuple-element.24.lists.lists_ref, f32[1,256]{1,0:T(1,128)S(1)} %get-tuple-element.31.resid.resid_ref, bf16[18,256,512]{2,1,0:T(8,128)(2,1)S(1)} %get-tuple-element.32.more_x2, s32[18,1,512]{2,1,0:T(1,128)S(1)} %get-tuple-element.33.more_hi), custom_call_target="tpu_custom_call" | custom-call | bytes 25165824 | tf_op jit(solution)/shard_map/pallas_call | solution.py:581
  24.9 13.9 %shard_map.89 = (f32[256,128]{1,0:T(8,128)S(1)}, f32[8,8,128]{2,1,0:T(8,128)S(1)}) custom-call(s32[24,128]{1,0:T(8,128)S(1)} %get-tuple-element.24.lists.lists_ref, f32[1024,256]{1,0:T(8,128)S(1)} %shard_map.88.rest_ref, f32[1,256]{1,0:T(1,128)S(1)} %get-tuple-element.31.resid.resid_ref, bf16[14,256,512]{2,1,0:T(8,128)(2,1)S(1)} %get-tuple-element.34.x2_ref, ...), custom_call_target="tpu_custom_call" | custom-call | bytes 25165824 | tf_op jit(solution)/shard_map/pallas_call | solution.py:590
  38.8 0.7 %shard_map.90 = (f32[1,256]{1,0:T(1,128)}, f32[256,128]{1,0:T(8,128)}, f32[1,1]{1,0:T(1,128)}) custom-call(f32[256,128]{1,0:T(8,128)S(1)} %get-tuple-element.40.sum_ref, f32[8,8,128]{2,1,0:T(8,128)S(1)} %get-tuple-element.41.notes_ref), custom_call_target="tpu_custom_call" | custom-call | bytes 25165824 | tf_op jit(solution)/shard_map/pallas_call | solution.py:617
Async XLA Ops:
  0.6 19.7 %copy-start = (s32[256]{0:T(256)S(1)}, s32[256]{0:T(256)}, u32[]{:S(2)}) copy-start(s32[256]{0:T(256)} %param.9) | copy-start | bytes 3076

commit v5 on v4

--- a/solution.py
+++ b/solution.py
@@ -363,8 +363,8 @@
     return jnp.concatenate(parts, axis=1)
 
 
-def late_kernel(grains, ready, lists, resid, more_x2, more_hi, total):
-    turns = lists[lists.shape[0] // 3 * 2, 0]
+def late_kernel(grains, ready, lists_ref, resid_ref, more_x2, more_hi, total, lists, resid, here):
+    hold = lists.shape[0] // 3
 
     def turn(t, carry):
         factor = jnp.broadcast_to(factor_row(grains, lists, resid, t), (8, WIDE))
@@ -373,10 +373,18 @@
             total[k : k + CUT, :] += spread_sum(x2, offset, factor, [k], CUT)
         return carry
 
-    @pl.when(turns > ready)
+    @pl.when(jnp.max(lists_ref[2 * hold :, :]) > ready)
     def _():
+        copies = [
+            pltpu.make_async_copy(lists_ref, lists, here.at[0]),
+            pltpu.make_async_copy(resid_ref, resid, here.at[1]),
+        ]
+        for copy in copies:
+            copy.start()
         total[...] = jnp.zeros_like(total)
-        lax.fori_loop(ready, turns, turn, jnp.int32(0))
+        for copy in copies:
+            copy.wait()
+        lax.fori_loop(ready, lists[2 * hold, 0], turn, jnp.int32(0))
 
 
 def scatter_kernel(
@@ -581,8 +589,9 @@
     rest = pl.pallas_call(
         functools.partial(late_kernel, grains, ready),
         out_shape=shape((deep * rows, 2 * width), f32),
-        in_specs=[SM, SM, VM, VM],
+        in_specs=[VM] * 4,
         out_specs=VM,
+        scratch_shapes=[pltpu.SMEM((3 * hold, LANES), i32), pltpu.SMEM((1, ex), f32), dma((2,))],
         compiler_params=pltpu.CompilerParams(vmem_limit_bytes=GRANT),
         cost_estimate=COST,
     )(lists, resid, more_x2, more_high)

time: 39.6 us -> 39 us (0.985)
  Pallas kernels: 38.8 us -> 38.2 us
    pallas_call x1, Pallas kernels: 0.75 us -> 0.22 us  [on_device(): pl.pallas_call(functools.partial(late_kernel, grains, ready), out_shape=s...]
where the time goes in v5:
time: 39 us; the launch traced here: 38.9 us
  Pallas kernels  38.2 us (98%)
  between operations  0.69 us (2%)
    pallas_call x1, Pallas kernels, on_device(): pl.pallas_call(functools.partial(gather_kernel, n), out_shape=(shape((n,...  18.7 us
    pallas_call x1, Pallas kernels, on_device(): pl.pallas_call(functools.partial(scatter_kernel, n, grains), out_shape=(s...  13.9 us
    pallas_call x1, Pallas kernels, on_device(): pl.pallas_call(functools.partial(residual_kernel, nf), out_shape=(shape((...  3.78 us
    pallas_call x1, Pallas kernels, on_device(): pl.pallas_call(margin_kernel, out_shape=(shape((8, ex), f32), shape((late...  0.96 us

profile of v5, /device:TPU:0, one launch (start us, length us, event | category | flops | bytes accessed | tf_op | source)
XLA Modules:
  0.0 38.9 jit_solution(2807943491417167828)
XLA Ops:
  0.6 0.0 copy-start
  0.6 18.7 %shard_map.85 = (bf16[8,256,128]{2,1,0:T(8,128)(2,1)S(1)}, bf16[14,256,512]{2,1,0:T(8,128)(2,1)S(1)}, s32[14,1,512]{2,1,0:T(1,128)S(1)}, s32[24,128]{1,0:T(8,128...) custom-call(f32[256,128]{1,0:T(8,128)} %w_hbm.1, ...), custom_call_target="tpu_custom_call" | custom-call | bytes 25165824 | tf_op jit(solution)/shard_map/pallas_call | solution.py:535
  19.4 1.0 %shard_map.86 = (f32[8,256]{1,0:T(8,128)S(1)}, bf16[18,256,512]{2,1,0:T(8,128)(2,1)S(1)}, s32[18,1,512]{2,1,0:T(1,128)S(1)}) custom-call(s32[24,128]{1,0:T(8,128)S(1)} %get-tuple-element.24.lists.lists_ref, bf16[8,256,128]{2,1,0:T(8,128)(2,1)S(1)} %get-tuple-element.25.table_ref, f32[256,128]{1,0:T(8,128)S(1)} %get-tuple-element.26.first_ref, ...), custom_call_target="tpu_custom_call" | custom-call | bytes 25165824 | tf_op jit(solution)/shard_map/pallas_call | solution.py:569
  20.4 0.0 copy-done
  20.4 3.8 %shard_map.87 = (f32[8,256]{1,0:T(8,128)S(1)}, f32[1,256]{1,0:T(1,128)S(1)}, f32[8,128]{1,0:T(8,128)S(1)}) custom-call(f32[8,256]{1,0:T(8,128)S(1)} %get-tuple-element.30.partial_ref, s32[1,256]{1,0:T(1,128)S(1)} %bitcast.7), custom_call_target="tpu_custom_call" | custom-call | bytes 25165824 | tf_op jit(solution)/shard_map/pallas_call | solution.py:579
  24.2 0.2 shard_map.88.rest_ref
  24.4 13.9 %shard_map.89 = (f32[256,128]{1,0:T(8,128)S(1)}, f32[8,8,128]{2,1,0:T(8,128)S(1)}) custom-call(s32[24,128]{1,0:T(8,128)S(1)} %get-tuple-element.24.lists.lists_ref, f32[1024,256]{1,0:T(8,128)S(1)} %shard_map.88.rest_ref, f32[1,256]{1,0:T(1,128)S(1)} %get-tuple-element.31.resid_ref, bf16[14,256,512]{2,1,0:T(8,128)(2,1)S(1)} %get-tuple-element.34.x2_ref, ...), custom_call_target="tpu_custom_call" | custom-call | bytes 25165824 | tf_op jit(solution)/shard_map/pallas_call | solution.py:599
  38.3 0.7 %shard_map.90 = (f32[1,256]{1,0:T(1,128)}, f32[256,128]{1,0:T(8,128)}, f32[1,1]{1,0:T(1,128)}) custom-call(f32[256,128]{1,0:T(8,128)S(1)} %get-tuple-element.40.sum_ref, f32[8,8,128]{2,1,0:T(8,128)S(1)} %get-tuple-element.41.notes_ref), custom_call_target="tpu_custom_call" | custom-call | bytes 25165824 | tf_op jit(solution)/shard_map/pallas_call | solution.py:626
Async XLA Ops:
  0.6 19.7 %copy-start = (s32[256]{0:T(256)S(1)}, s32[256]{0:T(256)}, u32[]{:S(2)}) copy-start(s32[256]{0:T(256)} %param.9) | copy-start | bytes 3076

commit v6 on v5

--- a/solution.py
+++ b/solution.py
@@ -242,16 +242,6 @@
     def crossing(z):
         return copy_to("rows", partner, half, table_ref.at[2 * z + 1 - side], send.at[0], xrecv.at[z])
 
-    near = far[::-1]
-    lax.fori_loop(0, x2_ref.shape[0] - steady, prepare_rest, jnp.int32(0), unroll=2)
-    for j, z in enumerate(near):
-        arrival(z).wait_recv()
-        block = table_ref.at[2 * z + side]
-        across.append(send_to("rows", partner, block, block, xsend.at[z], xrecv.at[z]))
-        if j == 0:
-            crossing(spot).wait_recv()
-            score(spot)
-
     local[3].wait()
     owner = own[...].astype(f32)
     square = jnp.broadcast_to(owner, (ex, ex))
@@ -262,6 +252,16 @@
     places = lax.broadcasted_iota(jnp.int32, (LANES, ex), 0).astype(f32)
     rank_ref[...] = jnp.where(places == rank, 1.0, 0.0)
     owner_ref[...] = jnp.broadcast_to(owner, owner_ref.shape)
+
+    near = far[::-1]
+    lax.fori_loop(0, x2_ref.shape[0] - steady, prepare_rest, jnp.int32(0), unroll=2)
+    for j, z in enumerate(near):
+        arrival(z).wait_recv()
+        block = table_ref.at[2 * z + side]
+        across.append(send_to("rows", partner, block, block, xsend.at[z], xrecv.at[z]))
+        if j == 0:
+            crossing(spot).wait_recv()
+            score(spot)
 
     for z in near:
         crossing(z).wait_recv()

time: 39 us -> 39 us (level)
  no operation moved by 1% of the time
where the time goes in v6:
time: 39 us; the launch traced here: 38.8 us
  Pallas kernels  38.1 us (98%)
  between operations  0.69 us (2%)
    pallas_call x1, Pallas kernels, on_device(): pl.pallas_call(functools.partial(gather_kernel, n), out_shape=(shape((n,...  18.7 us
    pallas_call x1, Pallas kernels, on_device(): pl.pallas_call(functools.partial(scatter_kernel, n, grains), out_shape=(s...  13.8 us
    pallas_call x1, Pallas kernels, on_device(): pl.pallas_call(functools.partial(residual_kernel, nf), out_shape=(shape((...  3.78 us
    pallas_call x1, Pallas kernels, on_device(): pl.pallas_call(margin_kernel, out_shape=(shape((8, ex), f32), shape((late...  0.96 us

profile of v6, /device:TPU:0, one launch (start us, length us, event | category | flops | bytes accessed | tf_op | source)
XLA Modules:
  0.0 38.8 jit_solution(13097719075858128908)
XLA Ops:
  0.6 0.0 copy-start
  0.6 18.7 %shard_map.85 = (bf16[8,256,128]{2,1,0:T(8,128)(2,1)S(1)}, bf16[14,256,512]{2,1,0:T(8,128)(2,1)S(1)}, s32[14,1,512]{2,1,0:T(1,128)S(1)}, s32[24,128]{1,0:T(8,128...) custom-call(f32[256,128]{1,0:T(8,128)} %w_hbm.1, ...), custom_call_target="tpu_custom_call" | custom-call | bytes 25165824 | tf_op jit(solution)/shard_map/pallas_call | solution.py:535
  19.4 1.0 %shard_map.86 = (f32[8,256]{1,0:T(8,128)S(1)}, bf16[18,256,512]{2,1,0:T(8,128)(2,1)S(1)}, s32[18,1,512]{2,1,0:T(1,128)S(1)}) custom-call(s32[24,128]{1,0:T(8,128)S(1)} %get-tuple-element.24.lists.lists_ref, bf16[8,256,128]{2,1,0:T(8,128)(2,1)S(1)} %get-tuple-element.25.table_ref, f32[256,128]{1,0:T(8,128)S(1)} %get-tuple-element.26.first_ref, ...), custom_call_target="tpu_custom_call" | custom-call | bytes 25165824 | tf_op jit(solution)/shard_map/pallas_call | solution.py:569
  20.4 0.0 copy-done
  20.4 3.8 %shard_map.87 = (f32[8,256]{1,0:T(8,128)S(1)}, f32[1,256]{1,0:T(1,128)S(1)}, f32[8,128]{1,0:T(8,128)S(1)}) custom-call(f32[8,256]{1,0:T(8,128)S(1)} %get-tuple-element.30.partial_ref, s32[1,256]{1,0:T(1,128)S(1)} %bitcast.7), custom_call_target="tpu_custom_call" | custom-call | bytes 25165824 | tf_op jit(solution)/shard_map/pallas_call | solution.py:579
  24.2 0.2 shard_map.88.rest_ref
  24.4 13.8 %shard_map.89 = (f32[256,128]{1,0:T(8,128)S(1)}, f32[8,8,128]{2,1,0:T(8,128)S(1)}) custom-call(s32[24,128]{1,0:T(8,128)S(1)} %get-tuple-element.24.lists.lists_ref, f32[1024,256]{1,0:T(8,128)S(1)} %shard_map.88.rest_ref, f32[1,256]{1,0:T(1,128)S(1)} %get-tuple-element.31.resid_ref, bf16[14,256,512]{2,1,0:T(8,128)(2,1)S(1)} %get-tuple-element.34.x2_ref, ...), custom_call_target="tpu_custom_call" | custom-call | bytes 25165824 | tf_op jit(solution)/shard_map/pallas_call | solution.py:599
  38.1 0.7 %shard_map.90 = (f32[1,256]{1,0:T(1,128)}, f32[256,128]{1,0:T(8,128)}, f32[1,1]{1,0:T(1,128)}) custom-call(f32[256,128]{1,0:T(8,128)S(1)} %get-tuple-element.40.sum_ref, f32[8,8,128]{2,1,0:T(8,128)S(1)} %get-tuple-element.41.notes_ref), custom_call_target="tpu_custom_call" | custom-call | bytes 25165824 | tf_op jit(solution)/shard_map/pallas_call | solution.py:626
Async XLA Ops:
  0.6 19.7 %copy-start = (s32[256]{0:T(256)S(1)}, s32[256]{0:T(256)}, u32[]{:S(2)}) copy-start(s32[256]{0:T(256)} %param.9) | copy-start | bytes 3076
